TPU v7x, 32 devices: a whole 2x2x4 slice. The times are simulated.
32 devices in a mesh: part: 2 (over x), col: 4 (over z), row: 4 (over y, core).
Axes of the slice: x: 2, y: 2, z: 4, core: 2. Of those that a mesh axis runs over, the one named last changes fastest.
Arguments:
- matrix: float32 [32768, 4, 48], P(('part', 'row'), 'col'), parts along dimension 0
Outputs:
- output 1: float32 [32768, 4, 48], P(('part', 'row'), 'col'), parts along dimension 0
- output 2: float32 [8, 48], P('part'), parts along dimension 0
- output 3: float32 [8, 48, 48], P('part'), parts along dimension 0
- output 4: float32 [32768, 192], P(('part', 'row')), parts along dimension 0
There are 2 independent parts. A program takes and returns all parts, laid end to end along the dimension named above; each array names one.
All inputs are finite; a program needn't handle non-finite values.
Results may differ from a plain program's by a relative error of at most 0.001.
Values sent between devices are 32-bit elements.
A program may use at most 1 GiB of HBM per device.

v0:
```python
import functools
import jax
import jax.numpy as jnp
from jax import lax
from jax.sharding import PartitionSpec as P

HIGHEST = lax.Precision.HIGHEST


def dot_high(lhs_mat, rhs_mat):
    return jnp.dot(lhs_mat, rhs_mat, precision=HIGHEST, preferred_element_type=jnp.float32)


def contract(einsum_form, lhs_mat, rhs_mat):
    return jnp.einsum(einsum_form, lhs_mat, rhs_mat, precision=HIGHEST, preferred_element_type=jnp.float32)


def factor_panel(panel_in, row_start, diag0, reduce_rows):
    rows_loc, panel_width = panel_in.shape
    global_rows = row_start + jnp.arange(rows_loc)
    col_ids = jnp.arange(panel_width)

    def column_step(col_step, carried):
        panel_work, refl_vecs, tau_vec = carried
        diag_row = diag0 + col_step
        column = lax.dynamic_index_in_dim(panel_work, col_step, axis=1, keepdims=False)
        x_col = jnp.where(global_rows >= diag_row, column, 0.0)
        local_row = diag_row - row_start
        holds_diag = (local_row >= 0) & (local_row < rows_loc)
        diag_row_vals = lax.dynamic_index_in_dim(panel_work, jnp.clip(local_row, 0, rows_loc - 1), axis=0, keepdims=False)
        diag_piece = jnp.where(holds_diag, diag_row_vals, 0.0)
        summed = reduce_rows(jnp.stack([dot_high(x_col, panel_work), diag_piece]))
        x_dots = summed[0]
        diag_vals = summed[1]
        alpha_val = diag_vals[col_step]
        col_norm = jnp.sqrt(x_dots[col_step])
        beta_val = jnp.where(alpha_val >= 0, -col_norm, col_norm)
        tau_step = (beta_val - alpha_val) / beta_val
        inv_scale = 1.0 / (alpha_val - beta_val)
        at_diag = global_rows == diag_row
        reflector = jnp.where(global_rows > diag_row, x_col * inv_scale, jnp.where(at_diag, 1.0, 0.0))
        v_dots = jnp.where(col_ids > col_step, inv_scale * (x_dots - alpha_val * diag_vals) + diag_vals, 0.0)
        panel_work = panel_work - tau_step * reflector[:, None] * v_dots[None, :]
        new_col = jnp.where(global_rows < diag_row, column, jnp.where(at_diag, beta_val, reflector))
        is_col = col_ids == col_step
        panel_work = jnp.where(is_col[None, :], new_col[:, None], panel_work)
        refl_vecs = jnp.where(is_col[None, :], reflector[:, None], refl_vecs)
        tau_vec = jnp.where(is_col, tau_step, tau_vec)
        return panel_work, refl_vecs, tau_vec

    init_carry = (panel_in, jnp.zeros_like(panel_in), jnp.zeros((panel_width,), jnp.float32))
    return lax.fori_loop(0, panel_width, column_step, init_carry)


def build_tfac(refl_vecs, tau_vec, reduce_rows):
    panel_width = tau_vec.shape[0]
    col_ids = jnp.arange(panel_width)
    gram_mat = reduce_rows(contract("rk,rl->kl", refl_vecs, refl_vecs))

    def t_step(col_step, t_fac):
        g_col = jnp.where(col_ids < col_step, lax.dynamic_index_in_dim(gram_mat, col_step, axis=1, keepdims=False), 0.0)
        tau_step = tau_vec[col_step]
        new_col = jnp.where(col_ids == col_step, tau_step, -tau_step * dot_high(t_fac, g_col))
        return jnp.where(col_ids[None, :] == col_step, new_col[:, None], t_fac)

    return lax.fori_loop(0, panel_width, t_step, jnp.zeros((panel_width, panel_width), jnp.float32))


def solution(mesh):
    proc_cols = mesh.shape["col"]
    sum_rows = functools.partial(lax.psum, axis_name="row")

    def local_program(a_loc):
        rows_loc, panels_loc, panel_width = a_loc.shape
        num_panels = panels_loc * proc_cols
        col_idx = lax.axis_index("col")
        row_start = lax.axis_index("row") * rows_loc
        global_rows = row_start + jnp.arange(rows_loc)
        panel_ids = jnp.arange(panels_loc) * proc_cols + col_idx

        def panel_step(panel_idx, carried):
            a_work, all_vecs, all_tfac = carried
            slot_idx = panel_idx // proc_cols
            is_owner = col_idx == panel_idx % proc_cols
            old_panel = lax.dynamic_index_in_dim(a_work, slot_idx, axis=1, keepdims=False)
            new_panel, refl_vecs, tau_vec = factor_panel(old_panel, row_start, panel_idx * panel_width, sum_rows)
            t_fac = build_tfac(refl_vecs, tau_vec, sum_rows)
            refl_vecs, t_fac = lax.psum((jnp.where(is_owner, refl_vecs, 0.0), jnp.where(is_owner, t_fac, 0.0)), "col")
            a_work = lax.dynamic_update_index_in_dim(a_work, jnp.where(is_owner, new_panel, old_panel), slot_idx, axis=1)
            proj_sum = sum_rows(contract("rk,rsj->ksj", refl_vecs, a_work))
            w_block = contract("kl,ksj->lsj", t_fac, proj_sum)
            w_block = jnp.where((panel_ids > panel_idx)[None, :, None], w_block, 0.0)
            a_work = a_work - contract("rl,lsj->rsj", refl_vecs, w_block)
            all_vecs = lax.dynamic_update_index_in_dim(all_vecs, refl_vecs, panel_idx, axis=0)
            all_tfac = lax.dynamic_update_index_in_dim(all_tfac, t_fac, panel_idx, axis=0)
            return a_work, all_vecs, all_tfac

        init_carry = (a_loc, jnp.zeros((num_panels, rows_loc, panel_width), jnp.float32), jnp.zeros((num_panels, panel_width, panel_width), jnp.float32))
        a_work, all_vecs, all_tfac = lax.fori_loop(0, num_panels, panel_step, init_carry)
        logical_cols = panel_ids[:, None] * panel_width + jnp.arange(panel_width)[None, :]
        q_init = (global_rows[:, None, None] == logical_cols[None, :, :]).astype(jnp.float32)

        def q_step(back_step, q_local):
            panel_idx = num_panels - 1 - back_step
            refl_vecs = lax.dynamic_index_in_dim(all_vecs, panel_idx, keepdims=False)
            t_fac = lax.dynamic_index_in_dim(all_tfac, panel_idx, keepdims=False)
            proj_sum = sum_rows(contract("rk,rsj->ksj", refl_vecs, q_local))
            w_block = contract("kl,lsj->ksj", t_fac, proj_sum)
            return q_local - contract("rk,ksj->rsj", refl_vecs, w_block)

        q_local = lax.fori_loop(0, num_panels, q_step, q_init)
        gathered = lax.all_gather(q_local, "col")
        q_rows = gathered.transpose(1, 2, 0, 3).reshape(rows_loc, num_panels * panel_width)
        tau_vals = jnp.diagonal(all_tfac, axis1=1, axis2=2)
        return a_work, tau_vals, all_tfac, q_rows

    spec_rows = P(("part", "row"), "col", None)
    out_specs = (spec_rows, P("part", None), P("part", None, None), P(("part", "row"), None))
    return jax.shard_map(local_program, mesh=mesh, in_specs=(spec_rows,), out_specs=out_specs, check_vma=False)
```

profile of v0, /device:TPU:0, one launch (start us, length us, event | category | flops | bytes accessed | tf_op | source)
XLA Modules:
  0.0 3668.8 jit_solution(16047966664230600264)
XLA Ops:
  11.1 3523.4 %while.128 = (s32[]{:T(128)}, f32[4096,1,48]{0,2,1:T(8,128)}, f32[4,4096,48]{1,2,0:T(8,128)}, f32[4,48,48]{2,1,0:T(8,128)S(1)}, s32[]{:T(128)}, /*index=5*/s32[]...) while((s32[]{:T(128)}, f32[4096,1,48]{0,2,1:T(8,128)}, ...), condition=%wide.region_10.11_spmd, body=%wide.region_0.10_spmd.sunk | while | flops 345503744 | bytes 28019188 | solution.py:99
  12.2 698.4 %while.130 = (s32[]{:T(128)}, f32[4096,48]{0,1:T(8,128)S(1)}, f32[4096,48]{0,1:T(8,128)}, f32[48]{0:T(128)S(1)}, s32[]{:T(128)}, /*index=5*/s32[]{:T(128)}, s32[...) while((s32[]{:T(128)}, f32[4096,48]{0,1:T(8,128)S(1)}, ...), condition=%wide.region_3.3_spmd.clone.clone.clone.clone, body=%wide.region_1.2_spmd.clone.clone.clone.clone.sunk | while | flops 3408609 | bytes 5755280 | solution.py:52
  13.6 8.4 psum.92
  159.4 6.5 psum.92
  713.6 42.7 %all-reduce.5.cloned.1.call-done = f32[4096,48]{0,1:T(8,128)} async-done(((f32[4096,48]{0,1:T(8,128)}), f32[4096,48]{0,1:T(8,128)}) %all-reduce.5.cloned.1.call-update) | async-done | bytes 786448 | tf_op jit(solution)/shard_map/while/body/eval_jaxpr/psum | solution.py:88
  758.5 11.6 all-reduce.2
  770.2 102.4 %while.131 = (s32[]{:T(128)}, f32[48,48]{1,0:T(8,128)S(1)}, f32[48]{0:T(128)S(1)}, f32[48,48]{0,1:T(8,128)S(1)}, s32[]{:T(128)}, /*index=5*/s32[]{:T(128)}) while((s32[]{:T(128)}, f32[48,48]{1,0:T(8,128)S(1)}, f32[48]{0:T(128)S(1)}, f32[48,48]{0,1:T(8,128)S(1)}, s32[]{:T(128)}, /*index=5*/s32[]{:T(128)}) %tuple.175), condition=%wide.region_7.7_spmd.clone.clone, body=%wide.region_6.6_spmd.clone.clone.sunk | while | flops 34852 | bytes 46156 | solution.py:66
  872.6 17.8 psum.90
  895.5 696.5 %while.130 = (s32[]{:T(128)}, f32[4096,48]{0,1:T(8,128)S(1)}, f32[4096,48]{0,1:T(8,128)}, f32[48]{0:T(128)S(1)}, s32[]{:T(128)}, /*index=5*/s32[]{:T(128)}, s32[...) while((s32[]{:T(128)}, f32[4096,48]{0,1:T(8,128)S(1)}, ...), condition=%wide.region_3.3_spmd.clone.clone.clone.clone, body=%wide.region_1.2_spmd.clone.clone.clone.clone.sunk | while | flops 3408609 | bytes 5755280 | solution.py:52
  1025.7 6.5 psum.92
  1594.2 41.8 %all-reduce.5.cloned.1.call-done = f32[4096,48]{0,1:T(8,128)} async-done(((f32[4096,48]{0,1:T(8,128)}), f32[4096,48]{0,1:T(8,128)}) %all-reduce.5.cloned.1.call-update) | async-done | bytes 786448 | tf_op jit(solution)/shard_map/while/body/eval_jaxpr/psum | solution.py:88
  1638.2 11.6 all-reduce.2
  1649.8 102.4 %while.131 = (s32[]{:T(128)}, f32[48,48]{1,0:T(8,128)S(1)}, f32[48]{0:T(128)S(1)}, f32[48,48]{0,1:T(8,128)S(1)}, s32[]{:T(128)}, /*index=5*/s32[]{:T(128)}) while((s32[]{:T(128)}, f32[48,48]{1,0:T(8,128)S(1)}, f32[48]{0:T(128)S(1)}, f32[48,48]{0,1:T(8,128)S(1)}, s32[]{:T(128)}, /*index=5*/s32[]{:T(128)}) %tuple.175), condition=%wide.region_7.7_spmd.clone.clone, body=%wide.region_6.6_spmd.clone.clone.sunk | while | flops 34852 | bytes 46156 | solution.py:66
  1752.2 17.8 psum.90
  1775.2 696.5 %while.130 = (s32[]{:T(128)}, f32[4096,48]{0,1:T(8,128)S(1)}, f32[4096,48]{0,1:T(8,128)}, f32[48]{0:T(128)S(1)}, s32[]{:T(128)}, /*index=5*/s32[]{:T(128)}, s32[...) while((s32[]{:T(128)}, f32[4096,48]{0,1:T(8,128)S(1)}, ...), condition=%wide.region_3.3_spmd.clone.clone.clone.clone, body=%wide.region_1.2_spmd.clone.clone.clone.clone.sunk | while | flops 3408609 | bytes 5755280 | solution.py:52
  1905.4 6.5 psum.92
  2473.8 41.8 %all-reduce.5.cloned.1.call-done = f32[4096,48]{0,1:T(8,128)} async-done(((f32[4096,48]{0,1:T(8,128)}), f32[4096,48]{0,1:T(8,128)}) %all-reduce.5.cloned.1.call-update) | async-done | bytes 786448 | tf_op jit(solution)/shard_map/while/body/eval_jaxpr/psum | solution.py:88
  2517.8 11.6 all-reduce.2
  2529.5 102.4 %while.131 = (s32[]{:T(128)}, f32[48,48]{1,0:T(8,128)S(1)}, f32[48]{0:T(128)S(1)}, f32[48,48]{0,1:T(8,128)S(1)}, s32[]{:T(128)}, /*index=5*/s32[]{:T(128)}) while((s32[]{:T(128)}, f32[48,48]{1,0:T(8,128)S(1)}, f32[48]{0:T(128)S(1)}, f32[48,48]{0,1:T(8,128)S(1)}, s32[]{:T(128)}, /*index=5*/s32[]{:T(128)}) %tuple.175), condition=%wide.region_7.7_spmd.clone.clone, body=%wide.region_6.6_spmd.clone.clone.sunk | while | flops 34852 | bytes 46156 | solution.py:66
  2631.9 17.8 psum.90
  2654.8 696.5 %while.130 = (s32[]{:T(128)}, f32[4096,48]{0,1:T(8,128)S(1)}, f32[4096,48]{0,1:T(8,128)}, f32[48]{0:T(128)S(1)}, s32[]{:T(128)}, /*index=5*/s32[]{:T(128)}, s32[...) while((s32[]{:T(128)}, f32[4096,48]{0,1:T(8,128)S(1)}, ...), condition=%wide.region_3.3_spmd.clone.clone.clone.clone, body=%wide.region_1.2_spmd.clone.clone.clone.clone.sunk | while | flops 3408609 | bytes 5755280 | solution.py:52
  2785.0 6.5 psum.92
  3353.5 42.9 %all-reduce.5.cloned.1.call-done = f32[4096,48]{0,1:T(8,128)} async-done(((f32[4096,48]{0,1:T(8,128)}), f32[4096,48]{0,1:T(8,128)}) %all-reduce.5.cloned.1.call-update) | async-done | bytes 786448 | tf_op jit(solution)/shard_map/while/body/eval_jaxpr/psum | solution.py:88
  3398.7 11.6 all-reduce.2
  3410.3 102.4 %while.131 = (s32[]{:T(128)}, f32[48,48]{1,0:T(8,128)S(1)}, f32[48]{0:T(128)S(1)}, f32[48,48]{0,1:T(8,128)S(1)}, s32[]{:T(128)}, /*index=5*/s32[]{:T(128)}) while((s32[]{:T(128)}, f32[48,48]{1,0:T(8,128)S(1)}, f32[48]{0:T(128)S(1)}, f32[48,48]{0,1:T(8,128)S(1)}, s32[]{:T(128)}, /*index=5*/s32[]{:T(128)}) %tuple.175), condition=%wide.region_7.7_spmd.clone.clone, body=%wide.region_6.6_spmd.clone.clone.sunk | while | flops 34852 | bytes 46156 | solution.py:66
  3512.7 17.8 psum.90
  3534.5 62.9 %while.129 = (s32[]{:T(128)}, f32[4096,1,48]{0,2,1:T(8,128)}, f32[4,4096,48]{1,2,0:T(8,128)}, f32[4,48,48]{2,1,0:T(8,128)S(1)}, s32[]{:T(128)}, /*index=5*/s32[]{:T(128)}, s32[]{:T(128)}, s32[]{:T(128)}) while((s32[]{:T(128)}, f32[4096,1,48]{0,2,1:T(8,128)}, f32[4,4096,48]{1,2,0:T(8,128)}, f32[4,48,48]{2,1,0:T(8,128)S(1)}, s32[]{:T(128)}, ...), condition=%wide.region_13.14_spmd, body=%wide.region_11.13_spmd.sunk | while | flops 228018432 | bytes 4027535 | solution.py:111
  3536.6 10.3 psum.91
  3552.3 10.3 psum.91
  3567.9 10.3 psum.91
  3583.5 10.6 psum.91
  3599.5 58.4 %all-gather.3.cloned.1.call-done = f32[16384,1,48]{0,2,1:T(8,128)} async-done(((f32[4096,1,48]{0,2,1:T(8,128)}), f32[16384,1,48]{0,2,1:T(8,128)}) %all-gather.3.cloned.1.call-update) | async-done | bytes 3145744 | tf_op jit(solution)/shard_map/all_gather | solution.py:112
  (4130 shorter events, 2473.2 us)
Async XLA Ops:
  11.1 745.2 %all-reduce.5.cloned.1.call-start = ((), (), s32[]{:S(2)}) async-start(), calls=%async_computation.1 | async-start | bytes 1572864 | tf_op jit(solution)/shard_map/while/body/eval_jaxpr/psum | solution.py:88
  710.6 2.2 copy-start
  756.3 134.3 %copy-start.1 = (f32[4096,48]{0,1:T(8,128)S(1)}, f32[4096,48]{0,1:T(8,128)}, u32[]{:S(2)}) copy-start(f32[4096,48]{0,1:T(8,128)} %all-reduce.5.cloned.1.call-done) | copy-start | bytes 2359300 | tf_op jit(solution)/shard_map/while
  894.4 741.6 %all-reduce.5.cloned.1.call-start = ((), (), s32[]{:S(2)}) async-start(), calls=%async_computation.1 | async-start | bytes 1572864 | tf_op jit(solution)/shard_map/while/body/eval_jaxpr/psum | solution.py:88
  1592.0 1.4 copy-start
  1636.0 134.3 %copy-start.1 = (f32[4096,48]{0,1:T(8,128)S(1)}, f32[4096,48]{0,1:T(8,128)}, u32[]{:S(2)}) copy-start(f32[4096,48]{0,1:T(8,128)} %all-reduce.5.cloned.1.call-done) | copy-start | bytes 2359300 | tf_op jit(solution)/shard_map/while
  1774.0 741.6 %all-reduce.5.cloned.1.call-start = ((), (), s32[]{:S(2)}) async-start(), calls=%async_computation.1 | async-start | bytes 1572864 | tf_op jit(solution)/shard_map/while/body/eval_jaxpr/psum | solution.py:88
  2471.7 1.4 copy-start
  2515.6 134.3 %copy-start.1 = (f32[4096,48]{0,1:T(8,128)S(1)}, f32[4096,48]{0,1:T(8,128)}, u32[]{:S(2)}) copy-start(f32[4096,48]{0,1:T(8,128)} %all-reduce.5.cloned.1.call-done) | copy-start | bytes 2359300 | tf_op jit(solution)/shard_map/while
  2653.7 742.7 %all-reduce.5.cloned.1.call-start = ((), (), s32[]{:S(2)}) async-start(), calls=%async_computation.1 | async-start | bytes 1572864 | tf_op jit(solution)/shard_map/while/body/eval_jaxpr/psum | solution.py:88
  3351.3 1.4 copy-start
  3396.4 134.3 %copy-start.1 = (f32[4096,48]{0,1:T(8,128)S(1)}, f32[4096,48]{0,1:T(8,128)}, u32[]{:S(2)}) copy-start(f32[4096,48]{0,1:T(8,128)} %all-reduce.5.cloned.1.call-done) | copy-start | bytes 2359300 | tf_op jit(solution)/shard_map/while
  3534.5 123.3 %all-gather.3.cloned.1.call-start = ((), (), s32[]{:S(2)}) async-start(), calls=%async_computation | async-start | bytes 3932160 | tf_op jit(solution)/shard_map/all_gather | solution.py:112
  3597.4 64.3 %copy-start.2 = (f32[4,48,48]{2,1,0:T(8,128)}, f32[4,48,48]{2,1,0:T(8,128)S(1)}, u32[]{:S(2)}) copy-start(f32[4,48,48]{2,1,0:T(8,128)S(1)} %get-tuple-element.1106) | copy-start | bytes 110596
Sparse Core Ops, SparseCore 0:
  713.0 43.2 all-reduce.4
  1593.1 42.7 all-reduce.4
  2472.8 42.7 all-reduce.4
  3352.4 43.9 all-reduce.4
Sparse Core Ops, SparseCore 1:
  3597.5 60.3 all-gather.2
where the time goes:
time: 3700 us; the launch traced here: 3670 us
  blocking collectives  1310 us (35%)
  loops' own time  760 us (21%)
  other arithmetic  653 us (18%)
  local copies, waits for them, and re-layouts  375 us (10%)
  matrix products  329 us (9%)
  waiting for transfers between devices  228 us (6%)
    psum x192, blocking collectives, column_step(): summed = reduce_rows(jnp.stack([dot_high(x_col, panel_work), diag_piece]))  1150 us
    another operation x4, loops' own time, factor_panel(): return lax.fori_loop(0, panel_width, column_step, init_carry)  634 us
    select_n x192, other arithmetic, column_step(): refl_vecs = jnp.where(is_col[None, :], reflector[:, None], refl_vecs)  470 us
    dot_general x384, matrix products, dot_high(): jnp.dot(lhs_mat, rhs_mat, precision=HIGHEST, preferred_element_type=jnp.f...  284 us
    psum x4, waiting for transfers between devices, panel_step(): lax.psum((jnp.where(is_owner, refl_vecs, 0.0), jnp.where(is_owner, t_fac,...  169 us
    mul x384, other arithmetic, column_step(): panel_work = panel_work - tau_step * reflector[:, None] * v_dots[None, :]  126 us
    another operation x4, loops' own time, build_tfac(): lax.fori_loop(0, panel_width, t_step, jnp.zeros((panel_width, panel_width...  126 us
    while x216, local copies, waits for them, and re-layouts  121 us

commit v1 on v0

--- a/solution.py
+++ b/solution.py
@@ -2,9 +2,469 @@
 import jax
 import jax.numpy as jnp
 from jax import lax
+from jax.experimental import pallas as pl
+from jax.experimental.pallas import tpu as pltpu
 from jax.sharding import PartitionSpec as P
 
 HIGHEST = lax.Precision.HIGHEST
+MESH = pl.DeviceIdType.MESH
+W = 48
+NP = 4
+N = W * NP
+NC = 8
+WIN = 4
+F32 = jnp.float32
+SUM_BOUND = 6144.0
+
+
+def mm(a, b):
+    return lax.dot_general(a, b, (((1,), (0,)), ((), ())), precision=HIGHEST, preferred_element_type=F32)
+
+
+def mm_nt(a, b):
+    return lax.dot_general(a, b, (((1,), (1,)), ((), ())), precision=HIGHEST, preferred_element_type=F32)
+
+
+def iota(shape, dim):
+    return lax.broadcasted_iota(jnp.int32, shape, dim)
+
+
+def roll(x, shift):
+    shift = shift % x.shape[1]
+    return x if shift == 0 else pltpu.roll(x, shift, 1)
+
+
+def widen(x, lanes):
+    return jnp.concatenate([x, jnp.zeros((x.shape[0], lanes - x.shape[1]), F32)], axis=1)
+
+
+def chain(limit, xc_ref, hn_ref, vt_ref, fr_ref, rn_ref, td_ref):
+    ng = W // 8
+    sub = iota((8, 128), 0)
+    lane = iota((8, 128), 1)
+    live0 = lane < limit
+    live1 = lane + 128 < limit
+    xs0 = [xc_ref[8 * s:8 * s + 8, 0:128] for s in range(ng)]
+    xs1 = [xc_ref[8 * s:8 * s + 8, 128:256] for s in range(ng)]
+    hs = [hn_ref[8 * s:8 * s + 8, :] for s in range(ng)]
+
+    def bcast_sub(x, u):
+        return jnp.broadcast_to(x[u:u + 1, :], (8, 128))
+
+    def bcast_col(x, k):
+        return jnp.broadcast_to(x[:, k:k + 1], (8, 128))
+
+    def columns(k):
+        return ({s: bcast_col(hs[s], k) for s in range(k // 8, ng)}, {s: bcast_col(xs0[s], k) for s in range(0, ng)})
+
+    window = {k: columns(k) for k in range(WIN)}
+    for k in range(W):
+        s0, u = k // 8, k % 8
+        ch, cx = window.pop(k)
+        hkk = bcast_sub(ch[s0], u)
+        alpha = bcast_sub(cx[s0], u)
+        inv_norm = lax.rsqrt(hkk)
+        inv_beta = jnp.where(alpha >= 0, -inv_norm, inv_norm)
+        beta = hkk * inv_beta
+        inv = 1.0 / (alpha - beta)
+        tau = (beta - alpha) * inv_beta
+        below = sub > u
+        rc, wc = {}, {}
+        for s in range(s0, ng):
+            r = ch[s] * inv_beta
+            w = cx[s] - r
+            rc[s] = jnp.where(below, r, 0.0) if s == s0 else r
+            wc[s] = jnp.where(below, w, 0.0) if s == s0 else w
+        r_of = {}
+        for m in range(k + 1, min(k + WIN, W)):
+            mh, mx = window[m]
+            r_m = bcast_sub(rc[m // 8], m % 8)
+            v_m = bcast_sub(mx[s0], u) * inv
+            for s in range(m // 8, ng):
+                mh[s] = mh[s] - rc[s] * r_m
+            for s in range(s0, ng):
+                mx[s] = mx[s] - wc[s] * v_m
+        hrow = bcast_sub(hs[s0], u) * inv_beta
+        x0 = bcast_sub(xs0[s0], u)
+        x1 = bcast_sub(xs1[s0], u)
+        s0v = x0 * inv
+        v0 = jnp.where(live0 & (lane > k), s0v, jnp.where(lane == k, 1.0, 0.0))
+        v1 = jnp.where(live1, x1 * inv, 0.0)
+        vt_ref[k:k + 1, 0:128] = v0[0:1, :]
+        vt_ref[k:k + 1, 128:256] = v1[0:1, :]
+        fr_ref[k:k + 1, 0:128] = jnp.where(live0 & (lane > k), s0v, jnp.where(lane == k, beta, x0))[0:1, :]
+        fr_ref[k:k + 1, 128:256] = jnp.where(live1, v1, x1)[0:1, :]
+        rn_ref[k:k + 1, :] = hrow[0:1, :]
+        td_ref[k:k + 1, :] = jnp.where(lane == k, tau, 0.0)[0:1, :]
+        for s in range(s0, ng):
+            hs[s] = hs[s] - rc[s] * hrow
+            xs0[s] = xs0[s] - wc[s] * v0
+            xs1[s] = xs1[s] - wc[s] * v1
+        if k + WIN < W:
+            window[k + WIN] = columns(k + WIN)
+
+
+def load_panel(g, refs):
+    xt, e1, e2, rts, wts, rinvd, rnat, kvt, xc_ref, hn_ref, dvec = (
+        refs["xt"], refs["e1"], refs["e2"], refs["rts"], refs["wts"], refs["rinvd"], refs["rnat"], refs["kv"], refs["xc"], refs["hn"], refs["dvec"])
+    x = xt[g]
+    lane = iota((W, 256), 1)
+    row = iota((W, 256), 0)
+    diag = jnp.sum(jnp.where(lane == row + N, x, 0.0), axis=0, keepdims=True)
+    dvec[0:1, :] = dvec[0:1, :] + roll(diag, 64 + W * g)
+    gram = roll(x, 64)[:, 0:128]
+    lane1 = lane[:, 0:128]
+    row1 = row[:, 0:128]
+    x = jnp.where(lane >= N, jnp.where(lane == row + N, 1.0, 0.0), x)
+    hgg = gram[:, 0:W]
+    for h in range(g):
+        if g - h == 1:
+            hgh = e1[g][:, 0:W]
+        elif g - h == 2:
+            hgh = roll(e1[g], 80)[:, 0:W]
+        else:
+            hgh = e2[0][:, 0:W] + e2[1][:, 0:W]
+        for q in range(h):
+            hgh = hgh - mm_nt(rts[g, q], rts[h, q])
+        rt = mm_nt(hgh, rinvd[h])
+        d = hgh - mm(x[:, 0:W], rnat[h])
+        both = mm(d, kvt[h])
+        x = roll(x - both[:, 0:256], 256 - W)
+        hgg = hgg - mm_nt(rt, rt)
+        rts[g, h] = rt
+        wts[g, h] = both[:, 256:256 + W]
+    xc_ref[...] = x
+    hn_ref[...] = jnp.where(lane1 < W, widen(hgg, 128), jnp.where(lane1 == row1 + 64, 1.0, 0.0))
+
+
+def close_panel(g, refs):
+    vt = refs["vt"][...]
+    fr = refs["fr"][...]
+    rn = refs["rn"][...]
+    td = refs["td"][...]
+    lane = iota((W, 256), 1)
+    lane1 = iota((W, 128), 1)
+    row1 = iota((W, 128), 0)
+    sq_lane = iota((W, W), 1)
+    sq_row = iota((W, W), 0)
+    refs["ftop"][g] = roll(fr, W * g)
+    mt = roll(vt, 64 + W * g)[:, 0:W]
+    v = jnp.where(lane < N - W * g, vt, 0.0)
+    rnat = jnp.where((lane1 >= row1) & (lane1 < W), rn, 0.0)[:, 0:W]
+    rinvt = roll(rn, 64)[:, 0:W]
+    rinvt = jnp.where(sq_lane <= sq_row, rinvt, 0.0)
+    mt = jnp.where(sq_lane <= sq_row, mt, 0.0)
+    refs["rnat"][g] = rnat
+    refs["rinvd"][g] = rinvt
+    s = -mm(v[:, 0:W], mm_nt(rnat, mt))
+    t = td[:, 0:W]
+    refs["tau"][g:g + 1, :] = jnp.sum(td, axis=0, keepdims=True)[:, 0:W]
+    size = 1
+    while size < W:
+        pair = (sq_row // (2 * size) == sq_lane // (2 * size)) & (sq_row // size < sq_lane // size)
+        t = t - mm(mm(t, jnp.where(pair, s, 0.0)), t)
+        size *= 2
+    refs["t"][g] = t
+    if g + 1 < NP:
+        kmat = lax.dot_general(mt, t, (((0,), (0,)), ((), ())), precision=HIGHEST, preferred_element_type=F32)
+        refs["kv"][g, :, 0:256] = mm(kmat, v)
+        refs["kv"][g, :, 256:384] = widen(kmat, 128)
+    lr = roll(widen(rinvt, 256), W * g)
+    lc = roll(widen(mt, 256), W * g)
+    if g:
+        rcat = sum(roll(widen(refs["rts"][g, h], 256), W * h) for h in range(g))
+        wcat = sum(roll(widen(refs["wts"][g, h], 256), W * h) for h in range(g))
+        lr = lr - mm(mm(rinvt, rcat)[:, 0:N], refs["lr"][...])
+        lc = lc - mm(mm(mt, wcat)[:, 0:N], refs["lc"][...])
+    refs["lr"][W * g:W * g + W, :] = lr
+    refs["lc"][W * g:W * g + W, :] = lc
+
+
+def fused_kernel(a_hbm, q_hbm, f_hbm, tau_ref, t_ref, flag_ref, panels, xt, e1, e2, x0s, x1s, x2s, x3s, g1s, g1r, g2s, g2r, h1s, h1r, h2s, h2r,
+                 rts, wts, rinvd, rnat, kvt, xc, hn, dvec, vt, fr, rn, td, ftop, lr, lc, lhs, q_stage, f_stage,
+                 load_sem, send_sem, bulk_sem, ex_send, ex_recv, e0_send, e0_recv, e1_send, e1_recv, e2_send, e2_recv, q_sem, f_sem):
+    refs = dict(xt=xt, e1=e1, e2=e2, rts=rts, wts=wts, rinvd=rinvd, rnat=rnat, kv=kvt, xc=xc, hn=hn, dvec=dvec,
+                vt=vt, fr=fr, rn=rn, td=td, ftop=ftop, lr=lr, lc=lc, tau=tau_ref, t=t_ref)
+    part = lax.axis_index("part")
+    c = lax.axis_index("col")
+    r = lax.axis_index("row")
+    width = panels.shape[3]
+    twin = r + 1 - 2 * lax.rem(r, 2)
+    across = lax.rem(r + 2, 4)
+
+    def at(col, row):
+        return (part, col, row)
+
+    for q in range(NC):
+        pltpu.make_async_copy(a_hbm.at[:, pl.ds(q * width, width)], panels.at[c, q], load_sem.at[q]).start()
+
+    barrier = pltpu.get_barrier_semaphore()
+    for s in range(1, NP):
+        pl.semaphore_signal(barrier, inc=1, device_id=at(lax.rem(c + s, NP), r), device_id_type=MESH)
+    pl.semaphore_signal(barrier, inc=1, device_id=at(c, twin), device_id_type=MESH)
+    pl.semaphore_signal(barrier, inc=1, device_id=at(c, across), device_id_type=MESH)
+    pl.semaphore_wait(barrier, NP + 1)
+
+    lr[...] = jnp.zeros_like(lr)
+    lc[...] = jnp.zeros_like(lc)
+    dvec[...] = jnp.zeros_like(dvec)
+    e2[...] = jnp.zeros_like(e2)
+
+    order_l = list(range(NC))
+    order_r = list(range(NC // 2, NC)) + list(range(NC // 2))
+
+    def bulk(side, g, q):
+        other = c - 1 if side == 0 else c + 1
+        return pltpu.make_async_remote_copy(
+            src_ref=panels.at[g, q], dst_ref=panels.at[g, q], send_sem=send_sem.at[side, g, q], recv_sem=bulk_sem.at[g, q],
+            device_id=at(other, r), device_id_type=MESH)
+
+    def start_own(i):
+        @pl.when(c >= 1)
+        def _():
+            bulk(0, c, order_l[i]).start()
+
+        @pl.when(c <= NP - 2)
+        def _():
+            bulk(1, c, order_r[i]).start()
+
+    def arrive(dist, i):
+        @pl.when(c + dist <= NP - 1)
+        def _():
+            bulk(0, c + dist, order_l[i]).wait_recv()
+
+        @pl.when(c - dist >= 0)
+        def _():
+            bulk(1, c - dist, order_r[i]).wait_recv()
+
+    def forward(dist, i):
+        @pl.when((c + dist <= NP - 1) & (c >= 1))
+        def _():
+            bulk(0, c + dist, order_l[i]).start()
+
+        @pl.when((c - dist >= 0) & (c <= NP - 2))
+        def _():
+            bulk(1, c - dist, order_r[i]).start()
+
+    def row_sum(e, mine, got1, half, got2, out, slot):
+        first = pltpu.make_async_remote_copy(mine, got1, ex_send.at[e, 0], ex_recv.at[e, 0], device_id=at(c, twin), device_id_type=MESH)
+        first.start()
+        first.wait()
+        half[...] = mine[...] + got1[...]
+        second = pltpu.make_async_remote_copy(half, got2, ex_send.at[e, 1], ex_recv.at[e, 1], device_id=at(c, across), device_id_type=MESH)
+        second.start()
+        second.wait()
+        out[slot] = half[...] + got2[...]
+
+    def shared(ref, slot, ssem, rsem, sslot, s, rslot):
+        return pltpu.make_async_remote_copy(ref.at[slot], ref.at[slot], ssem.at[sslot], rsem.at[rslot],
+                                            device_id=at(lax.rem(c + s, NP), r), device_id_type=MESH)
+
+    def chunk_cols(g, q):
+        return panels[g, q]
+
+    for q in range(NC):
+        pltpu.make_async_copy(a_hbm.at[:, pl.ds(q * width, width)], panels.at[c, q], load_sem.at[q]).wait()
+    head = 3
+    for i in range(head):
+        start_own(i)
+    gram = jnp.zeros((W, W), F32)
+    for q in range(NC):
+        blk = chunk_cols(c, q)
+        gram = gram + mm_nt(blk, blk)
+    lane = iota((W, 256), 1)
+    top = jnp.where((lane < N) & (r == 0), panels[c, 0, :, 0:256], 0.0)
+    x0s[...] = top + roll(widen(gram, 256), N)
+    row_sum(0, x0s, x1s, x2s, x3s, xt, c)
+    for s in range(1, NP):
+        shared(xt, c, e0_send, e0_recv, s - 1, s, c).start()
+    for i in range(head, NC):
+        start_own(i)
+
+    def wait_e0(g):
+        @pl.when(c != g)
+        def _():
+            shared(xt, g, e0_send, e0_recv, 0, 1, g).wait_recv()
+
+    def wait_e1(g):
+        @pl.when(c != g - 1)
+        def _():
+            shared(e1, g, e1_send, e1_recv, 0, 1, g).wait_recv()
+
+    def wait_e2(i):
+        @pl.when(c != i + 1)
+        def _():
+            shared(e2, i, e2_send, e2_recv, 0, 1, i).wait_recv()
+
+    def before(g):
+        if g == 0:
+            wait_e0(0)
+        if g == 1:
+            for i in range(NC):
+                arrive(1, i)
+                if i < head:
+                    forward(1, i)
+
+            @pl.when(c <= NP - 2)
+            def _():
+                left = jnp.maximum(c - 1, 0)
+                acc = jnp.zeros((W, 2 * W), F32)
+                for q in range(NC):
+                    pair = jnp.concatenate([chunk_cols(c, q), chunk_cols(left, q)], axis=0)
+                    acc = acc + mm_nt(chunk_cols(c + 1, q), pair)
+                g1s[...] = widen(acc, 128)
+                row_sum(1, g1s, g1r, g2s, g2r, e1, c + 1)
+                for s in range(1, NP):
+                    shared(e1, c + 1, e1_send, e1_recv, s - 1, s, c + 1).start()
+            for i in range(head, NC):
+                forward(1, i)
+            wait_e0(1)
+            wait_e1(1)
+        if g == 2:
+            half = NC // 2
+            for i in range(half):
+                arrive(2, i)
+                if i < 1:
+                    forward(2, i)
+
+            @pl.when((c >= 1) & (c <= 2))
+            def _():
+                base = (c - 1) * half
+                acc = jnp.zeros((W, W), F32)
+                for i in range(half):
+                    acc = acc + mm_nt(chunk_cols(3, base + i), chunk_cols(0, base + i))
+                h1s[...] = widen(acc, 128)
+                row_sum(2, h1s, h1r, h2s, h2r, e2, c - 1)
+                for s in range(1, NP):
+                    shared(e2, c - 1, e2_send, e2_recv, s - 1, s, c - 1).start()
+            for i in range(1, half):
+                forward(2, i)
+            wait_e0(2)
+            wait_e1(2)
+        if g == 3:
+            for i in range(NC // 2, NC):
+                arrive(2, i)
+                forward(2, i)
+            wait_e0(3)
+            wait_e1(3)
+            wait_e2(0)
+            wait_e2(1)
+
+    def panel_step(g, carry):
+        for s in range(NP):
+            @pl.when(g == s)
+            def _():
+                before(s)
+                load_panel(s, refs)
+        chain(256 - W * g, xc, hn, vt, fr, rn, td)
+        for s in range(NP):
+            @pl.when(g == s)
+            def _():
+                close_panel(s, refs)
+        return carry
+
+    lax.fori_loop(0, NP, panel_step, 0)
+
+    dv = dvec[0:1, 0:N]
+    lr_all = lr[...][:, 0:N]
+    lc_all = lc[...][:, 0:N]
+    good = ((jnp.sum(lr_all * lr_all * dv) <= SUM_BOUND) & (jnp.sum(lc_all * lc_all * dv) <= SUM_BOUND)
+            & (jnp.min(dv) > 1e-18) & (jnp.max(dv) < 1e30))
+    flag_ref[...] = jnp.zeros((8, 128), F32) + jnp.where(good, 0.0, 1.0)
+
+    lhs[0:N, :] = lr[...]
+    lhs[N:N + W, :] = lc[pl.ds(pl.multiple_of(c * W, W), W), :]
+    ftop_c = ftop[c]
+
+    def out_copies(slot, q):
+        cols = pl.ds(pl.multiple_of(q * width, width), width)
+        return (pltpu.make_async_copy(q_stage.at[slot], q_hbm.at[:, cols], q_sem.at[slot]),
+                pltpu.make_async_copy(f_stage.at[slot], f_hbm.at[:, cols], f_sem.at[slot]))
+
+    def out_step(i, carry):
+        q = lax.rem(i + jnp.where(c >= 2, NC // 2, 0), NC)
+        slot = lax.rem(i, 2)
+
+        @pl.when(c == 0)
+        def _():
+            bulk(0, 3, q).wait_recv()
+
+        @pl.when(c == NP - 1)
+        def _():
+            bulk(1, 0, q).wait_recv()
+
+        @pl.when(i >= 2)
+        def _():
+            for cp in out_copies(slot, q):
+                cp.wait()
+        rhs = jnp.concatenate([panels[g, q] for g in range(NP)], axis=0)
+        prod = mm(lhs[:, 0:N], rhs)
+        q_stage[slot] = prod[0:N]
+        f_stage[slot] = prod[N:N + W]
+
+        @pl.when((q == 0) & (r == 0))
+        def _():
+            keep = iota((W, 256), 1) < N
+            f_stage[slot, :, 0:256] = jnp.where(keep, ftop_c, prod[N:N + W, 0:256])
+        for cp in out_copies(slot, q):
+            cp.start()
+        return carry
+
+    lax.fori_loop(0, NC, out_step, 0)
+    for slot in range(2):
+        for cp in out_copies(slot, 0):
+            cp.wait()
+
+    for i in range(NC):
+        @pl.when(c >= 1)
+        def _():
+            for s in range(NP):
+                @pl.when(c <= s)
+                def _():
+                    bulk(0, s, i).wait_send()
+
+        @pl.when(c <= NP - 2)
+        def _():
+            for s in range(NP):
+                @pl.when(c >= s)
+                def _():
+                    bulk(1, s, i).wait_send()
+    for s in range(1, NP):
+        shared(xt, c, e0_send, e0_recv, s - 1, s, c).wait_send()
+
+        @pl.when(c <= NP - 2)
+        def _():
+            shared(e1, c + 1, e1_send, e1_recv, s - 1, s, c + 1).wait_send()
+
+        @pl.when((c >= 1) & (c <= 2))
+        def _():
+            shared(e2, c - 1, e2_send, e2_recv, s - 1, s, c - 1).wait_send()
+
+
+def fused_qr(a_t):
+    rows = a_t.shape[1]
+    width = rows // NC
+    vm = lambda *shape: pltpu.VMEM(shape, F32)
+    dma = lambda *shape: pltpu.SemaphoreType.DMA(shape)
+    out = lambda *shape: jax.ShapeDtypeStruct(shape, F32)
+    hbm = pl.BlockSpec(memory_space=pl.ANY)
+    vmem = pl.BlockSpec(memory_space=pltpu.VMEM)
+    scratch = [vm(NP, NC, W, width), vm(NP, W, 256), vm(NP, W, 128), vm(2, W, 128), vm(W, 256), vm(W, 256), vm(W, 256)]
+    scratch += [vm(W, 256)]
+    scratch += [vm(W, 128)] * 8
+    scratch += [vm(NP, 3, W, W), vm(NP, 3, W, W), vm(NP, W, W), vm(NP, W, W), vm(3, W, 384), vm(W, 256), vm(W, 128), vm(8, 256),
+                vm(W, 256), vm(W, 256), vm(W, 128), vm(W, 128), vm(NP, W, 256), vm(N, 256), vm(N, 256), vm(N + W, 256),
+                vm(2, N, width), vm(2, W, width)]
+    scratch += [dma(NC), dma(2, NP, NC), dma(NP, NC), dma(3, 2), dma(3, 2), dma(3), dma(NP), dma(3), dma(NP), dma(3), dma(2), dma(2), dma(2)]
+    return pl.pallas_call(
+        fused_kernel,
+        name="fused_qr",
+        out_shape=(out(N, rows), out(W, rows), out(NP, W), out(NP, W, W), out(8, 128)),
+        in_specs=[hbm],
+        out_specs=(hbm, hbm, vmem, vmem, vmem),
+        scratch_shapes=scratch,
+        compiler_params=pltpu.CompilerParams(collective_id=0, has_side_effects=True, vmem_limit_bytes=32 * 1024 * 1024),
+    )(a_t)
 
 
 def dot_high(lhs_mat, rhs_mat):
@@ -66,8 +526,7 @@
     return lax.fori_loop(0, panel_width, t_step, jnp.zeros((panel_width, panel_width), jnp.float32))
 
 
-def solution(mesh):
-    proc_cols = mesh.shape["col"]
+def careful_program(proc_cols):
     sum_rows = functools.partial(lax.psum, axis_name="row")
 
     def local_program(a_loc):
@@ -114,6 +573,23 @@
         tau_vals = jnp.diagonal(all_tfac, axis1=1, axis2=2)
         return a_work, tau_vals, all_tfac, q_rows
 
+    return local_program
+
+
+def solution(mesh):
+    careful = careful_program(mesh.shape["col"])
+
+    def local_program(a_loc):
+        rows_loc = a_loc.shape[0]
+        q_t, f_t, tau_vals, t_fac, flag = fused_qr(a_loc.reshape(rows_loc, W).T)
+
+        def again(state):
+            factored, tau_new, t_new, q_new = careful(a_loc)
+            return jnp.float32(0.0), factored, tau_new, t_new, q_new
+
+        state = (flag[0, 0], f_t.T.reshape(rows_loc, 1, W), tau_vals, t_fac, q_t.T)
+        return lax.while_loop(lambda s: s[0] > 0.5, again, state)[1:]
+
     spec_rows = P(("part", "row"), "col", None)
     out_specs = (spec_rows, P("part", None), P("part", None, None), P(("part", "row"), None))
     return jax.shard_map(local_program, mesh=mesh, in_specs=(spec_rows,), out_specs=out_specs, check_vma=False)

time: 3700 us -> 93.2 us (0.03)
  blocking collectives: 1310 us -> 0 us
  loops' own time: 760 us -> 0.83 us
  other arithmetic: 653 us -> 0 us
  local copies, waits for them, and re-layouts: 375 us -> 10.1 us
  matrix products: 329 us -> 0 us
  waiting for transfers between devices: 228 us -> 0 us
  Pallas kernels: 0 us -> 67.9 us
    psum x204 -> x0, blocking collectives: 1310 us -> none  [the longest x192 1150 us: column_step(): summed = reduce_rows(jnp.stack([dot_high(x_col, panel_work), diag_piece]))]
    another operation x10 -> x1, loops' own time: 760 us -> 0.83 us  [local_program(): return lax.while_loop(lambda s: s[0] > 0.5, again, state)[1:]]
    select_n x1160 -> x0, other arithmetic: 512 us -> none  [the longest x192 470 us: column_step(): refl_vecs = jnp.where(is_col[None, :], reflector[:, None], refl_vecs)]
    dot_general x412 -> x0, matrix products: 329 us -> none  [the longest x384 284 us: dot_high(): jnp.dot(lhs_mat, rhs_mat, precision=HIGHEST, preferred_element_type=jnp.f...]
    dynamic_slice x576 -> x0, local copies, waits for them, and re-layouts: 241 us -> none  [the longest x192 120 us: column_step(): alpha_val = diag_vals[col_step]]
    psum x4 -> x0, waiting for transfers between devices: 169 us -> none  [panel_step(): lax.psum((jnp.where(is_owner, refl_vecs, 0.0), jnp.where(is_owner, t_fac,...]
    mul x384 -> x0, other arithmetic: 126 us -> none  [column_step(): panel_work = panel_work - tau_step * reflector[:, None] * v_dots[None, :]]
    while x217 -> x1, local copies, waits for them, and re-layouts: 121 us -> 0.7 us  [local_program(): return lax.while_loop(lambda s: s[0] > 0.5, again, state)[1:]]
where the time goes in v1:
time: 93.2 us; the launch traced here: 92.9 us
  Pallas kernels  67.9 us (73%)
  between operations  14 us (15%)
  local copies, waits for them, and re-layouts  10.1 us (11%)
    pallas_call x1, Pallas kernels, fused_qr(): pl.pallas_call(fused_kernel, name='fused_qr', out_shape=(out(N, rows), ou...  67.9 us
    unnamed x4, local copies, waits for them, and re-layouts  8.85 us

profile of v1, /device:TPU:0, one launch (start us, length us, event | category | flops | bytes accessed | tf_op | source)
XLA Modules:
  0.0 92.9 jit_solution(11423855787024523046)
XLA Ops:
  7.2 67.9 %fused_qr.1 = (f32[192,4096]{1,0:T(8,128)}, f32[48,4096]{1,0:T(8,128)}, f32[4,48]{1,0:T(4,128)S(1)}, f32[4,48,48]{2,1,0:T(8,128)}, f32[8,128]{1,0:T(8,128)S(1)}) custom-call(f32[48,4096]{1,0:T(8,128)} %bitcast.167), custom_call_target="tpu_custom_call" | custom-call | tf_op jit(solution)/shard_map/fused_qr/pallas_call | solution.py:459
  75.1 0.5 slice.17
  75.6 0.7 copy.27
  76.3 0.8 while.131
  77.2 1.4 %copy.28 = f32[4,48]{1,0:T(4,128)} copy(f32[4,48]{0,1:T(8,128)} %get-tuple-element.784) | data formatting | bytes 1536
  78.6 2.1 %copy.95 = f32[4096,1,48]{0,2,1:T(8,128)} copy(f32[4096,1,48]{0,2,1:T(8,128)} %get-tuple-element.1208) | data formatting | bytes 1572864
  80.6 1.5 %copy.96 = f32[4,48,48]{2,1,0:T(8,128)} copy(f32[4,48,48]{2,1,0:T(8,128)} %get-tuple-element.1210) | data formatting | bytes 73728
  82.2 3.9 %copy.97 = f32[4096,192]{0,1:T(8,128)} copy(f32[4096,192]{0,1:T(8,128)} %get-tuple-element.1211) | data formatting | bytes 6291456

commit v2 on v1

--- a/solution.py
+++ b/solution.py
@@ -15,6 +15,12 @@
 WIN = 4
 F32 = jnp.float32
 SUM_BOUND = 6144.0
+STEPS = 8
+AUX_TOP = N + W
+AUX_T = AUX_TOP + W
+AUX_TAU = AUX_T + N
+AUX_MODE = AUX_TAU + 8
+AUX_ROWS = AUX_MODE + 8
 
 
 def mm(a, b):
@@ -180,11 +186,11 @@
     refs["lc"][W * g:W * g + W, :] = lc
 
 
-def fused_kernel(a_hbm, q_hbm, f_hbm, tau_ref, t_ref, flag_ref, panels, xt, e1, e2, x0s, x1s, x2s, x3s, g1s, g1r, g2s, g2r, h1s, h1r, h2s, h2r,
-                 rts, wts, rinvd, rnat, kvt, xc, hn, dvec, vt, fr, rn, td, ftop, lr, lc, lhs, q_stage, f_stage,
-                 load_sem, send_sem, bulk_sem, ex_send, ex_recv, e0_send, e0_recv, e1_send, e1_recv, e2_send, e2_recv, q_sem, f_sem):
+def gather_kernel(a_hbm, b_hbm, f_alt, aux_ref, flag_ref, panels, xt, e1, e2, x0s, x1s, x2s, x3s, g1s, g1r, g2s, g2r, h1s, h1r, h2s, h2r,
+                 rts, wts, rinvd, rnat, kvt, xc, hn, dvec, vt, fr, rn, td, ftop, lr, lc, tau, t_fac, bad_mine, bad_other,
+                 load_sem, send_sem, bulk_sem, ex_send, ex_recv, e0_send, e0_recv, e1_send, e1_recv, e2_send, e2_recv, flag_sem, write_sem):
     refs = dict(xt=xt, e1=e1, e2=e2, rts=rts, wts=wts, rinvd=rinvd, rnat=rnat, kv=kvt, xc=xc, hn=hn, dvec=dvec,
-                vt=vt, fr=fr, rn=rn, td=td, ftop=ftop, lr=lr, lc=lc, tau=tau_ref, t=t_ref)
+                vt=vt, fr=fr, rn=rn, td=td, ftop=ftop, lr=lr, lc=lc, tau=tau, t=t_fac)
     part = lax.axis_index("part")
     c = lax.axis_index("col")
     r = lax.axis_index("row")
@@ -203,7 +209,8 @@
         pl.semaphore_signal(barrier, inc=1, device_id=at(lax.rem(c + s, NP), r), device_id_type=MESH)
     pl.semaphore_signal(barrier, inc=1, device_id=at(c, twin), device_id_type=MESH)
     pl.semaphore_signal(barrier, inc=1, device_id=at(c, across), device_id_type=MESH)
-    pl.semaphore_wait(barrier, NP + 1)
+    pl.semaphore_signal(barrier, inc=1, device_id=(1 - part, c, r), device_id_type=MESH)
+    pl.semaphore_wait(barrier, NP + 2)
 
     lr[...] = jnp.zeros_like(lr)
     lc[...] = jnp.zeros_like(lc)
@@ -228,14 +235,19 @@
         def _():
             bulk(1, c, order_r[i]).start()
 
+    def write(g, q):
+        return pltpu.make_async_copy(panels.at[g, q], b_hbm.at[pl.ds(pl.multiple_of(g * W, W), W), pl.ds(q * width, width)], write_sem.at[g, q])
+
     def arrive(dist, i):
         @pl.when(c + dist <= NP - 1)
         def _():
             bulk(0, c + dist, order_l[i]).wait_recv()
+            write(c + dist, order_l[i]).start()
 
         @pl.when(c - dist >= 0)
         def _():
             bulk(1, c - dist, order_r[i]).wait_recv()
+            write(c - dist, order_r[i]).start()
 
     def forward(dist, i):
         @pl.when((c + dist <= NP - 1) & (c >= 1))
@@ -268,6 +280,8 @@
     head = 3
     for i in range(head):
         start_own(i)
+    for q in range(NC):
+        write(c, q).start()
     gram = jnp.zeros((W, W), F32)
     for q in range(NC):
         blk = chunk_cols(c, q)
@@ -370,50 +384,25 @@
     lc_all = lc[...][:, 0:N]
     good = ((jnp.sum(lr_all * lr_all * dv) <= SUM_BOUND) & (jnp.sum(lc_all * lc_all * dv) <= SUM_BOUND)
             & (jnp.min(dv) > 1e-18) & (jnp.max(dv) < 1e30))
-    flag_ref[...] = jnp.zeros((8, 128), F32) + jnp.where(good, 0.0, 1.0)
-
-    lhs[0:N, :] = lr[...]
-    lhs[N:N + W, :] = lc[pl.ds(pl.multiple_of(c * W, W), W), :]
-    ftop_c = ftop[c]
-
-    def out_copies(slot, q):
-        cols = pl.ds(pl.multiple_of(q * width, width), width)
-        return (pltpu.make_async_copy(q_stage.at[slot], q_hbm.at[:, cols], q_sem.at[slot]),
-                pltpu.make_async_copy(f_stage.at[slot], f_hbm.at[:, cols], f_sem.at[slot]))
-
-    def out_step(i, carry):
-        q = lax.rem(i + jnp.where(c >= 2, NC // 2, 0), NC)
-        slot = lax.rem(i, 2)
-
-        @pl.when(c == 0)
-        def _():
-            bulk(0, 3, q).wait_recv()
-
-        @pl.when(c == NP - 1)
-        def _():
-            bulk(1, 0, q).wait_recv()
-
-        @pl.when(i >= 2)
-        def _():
-            for cp in out_copies(slot, q):
-                cp.wait()
-        rhs = jnp.concatenate([panels[g, q] for g in range(NP)], axis=0)
-        prod = mm(lhs[:, 0:N], rhs)
-        q_stage[slot] = prod[0:N]
-        f_stage[slot] = prod[N:N + W]
-
-        @pl.when((q == 0) & (r == 0))
-        def _():
-            keep = iota((W, 256), 1) < N
-            f_stage[slot, :, 0:256] = jnp.where(keep, ftop_c, prod[N:N + W, 0:256])
-        for cp in out_copies(slot, q):
-            cp.start()
-        return carry
-
-    lax.fori_loop(0, NC, out_step, 0)
-    for slot in range(2):
-        for cp in out_copies(slot, 0):
-            cp.wait()
+    bad_mine[...] = jnp.zeros((8, 128), F32) + jnp.where(good, 0.0, 1.0)
+    flag_copy = pltpu.make_async_remote_copy(bad_mine, bad_other, flag_sem.at[0], flag_sem.at[1], device_id=(1 - part, c, r), device_id_type=MESH)
+    flag_copy.start()
+
+    aux_ref[0:N, :] = lr[...]
+    aux_ref[N:N + W, :] = lc[pl.ds(pl.multiple_of(c * W, W), W), :]
+    aux_ref[AUX_TOP:AUX_TOP + W, :] = ftop[c]
+    for g in range(NP):
+        aux_ref[AUX_T + W * g:AUX_T + W * g + W, :] = widen(t_fac[g], 256)
+    aux_ref[AUX_TAU:AUX_TAU + 8, :] = jnp.concatenate([widen(tau[...], 256), jnp.zeros((4, 256), F32)], axis=0)
+    aux_ref[AUX_MODE:AUX_MODE + 8, :] = jnp.zeros((8, 256), F32)
+
+    for i in range(NC):
+        arrive(3, i)
+    flag_copy.wait()
+    flag_ref[0] = jnp.max(jnp.maximum(bad_mine[...], bad_other[...]))
+    for g in range(NP):
+        for q in range(NC):
+            write(g, q).wait()
 
     for i in range(NC):
         @pl.when(c >= 1)
@@ -441,30 +430,102 @@
             shared(e2, c - 1, e2_send, e2_recv, s - 1, s, c - 1).wait_send()
 
 
-def fused_qr(a_t):
+def gather_and_factor(a_t):
     rows = a_t.shape[1]
     width = rows // NC
     vm = lambda *shape: pltpu.VMEM(shape, F32)
     dma = lambda *shape: pltpu.SemaphoreType.DMA(shape)
     out = lambda *shape: jax.ShapeDtypeStruct(shape, F32)
     hbm = pl.BlockSpec(memory_space=pl.ANY)
-    vmem = pl.BlockSpec(memory_space=pltpu.VMEM)
     scratch = [vm(NP, NC, W, width), vm(NP, W, 256), vm(NP, W, 128), vm(2, W, 128), vm(W, 256), vm(W, 256), vm(W, 256)]
     scratch += [vm(W, 256)]
     scratch += [vm(W, 128)] * 8
     scratch += [vm(NP, 3, W, W), vm(NP, 3, W, W), vm(NP, W, W), vm(NP, W, W), vm(3, W, 384), vm(W, 256), vm(W, 128), vm(8, 256),
-                vm(W, 256), vm(W, 256), vm(W, 128), vm(W, 128), vm(NP, W, 256), vm(N, 256), vm(N, 256), vm(N + W, 256),
-                vm(2, N, width), vm(2, W, width)]
-    scratch += [dma(NC), dma(2, NP, NC), dma(NP, NC), dma(3, 2), dma(3, 2), dma(3), dma(NP), dma(3), dma(NP), dma(3), dma(2), dma(2), dma(2)]
+                vm(W, 256), vm(W, 256), vm(W, 128), vm(W, 128), vm(NP, W, 256), vm(N, 256), vm(N, 256),
+                vm(NP, W), vm(NP, W, W), vm(8, 128), vm(8, 128)]
+    scratch += [dma(NC), dma(2, NP, NC), dma(NP, NC), dma(3, 2), dma(3, 2), dma(3), dma(NP), dma(3), dma(NP), dma(3), dma(2), dma(2), dma(NP, NC)]
     return pl.pallas_call(
-        fused_kernel,
-        name="fused_qr",
-        out_shape=(out(N, rows), out(W, rows), out(NP, W), out(NP, W, W), out(8, 128)),
+        gather_kernel,
+        name="gather_and_factor",
+        out_shape=(out(N, rows), out(W, rows), out(AUX_ROWS, 256), out(1)),
         in_specs=[hbm],
-        out_specs=(hbm, hbm, vmem, vmem, vmem),
+        out_specs=(hbm, hbm, pl.BlockSpec(memory_space=pltpu.VMEM), pl.BlockSpec(memory_space=pltpu.SMEM)),
         scratch_shapes=scratch,
         compiler_params=pltpu.CompilerParams(collective_id=0, has_side_effects=True, vmem_limit_bytes=32 * 1024 * 1024),
     )(a_t)
+
+
+def pack_kernel(tau_ref, t_ref, aux_ref):
+    aux_ref[...] = jnp.zeros_like(aux_ref)
+    for g in range(NP):
+        aux_ref[AUX_T + W * g:AUX_T + W * g + W, 0:W] = t_ref[g]
+    aux_ref[AUX_TAU:AUX_TAU + NP, 0:W] = tau_ref[...]
+    aux_ref[AUX_MODE:AUX_MODE + 8, :] = jnp.ones((8, 256), F32)
+
+
+def pack_aux(tau_vals, t_fac):
+    return pl.pallas_call(pack_kernel, name="pack_aux", out_shape=jax.ShapeDtypeStruct((AUX_ROWS, 256), F32))(tau_vals, t_fac)
+
+
+def product_kernel(b_ref, f_alt, aux_ref, q_ref, f_ref, tau_ref, t_ref, sem):
+    step = pl.program_id(0)
+    width = b_ref.shape[1]
+    careful = jnp.max(aux_ref[AUX_MODE:AUX_MODE + 8, 0:128]) > 0.5
+
+    @pl.when(step == 0)
+    def _():
+        tau_ref[...] = aux_ref[AUX_TAU:AUX_TAU + NP, 0:W]
+        for g in range(NP):
+            t_ref[g] = aux_ref[AUX_T + W * g:AUX_T + W * g + W, 0:W]
+
+    @pl.when(jnp.logical_not(careful))
+    def _():
+        prod = mm(aux_ref[0:N + W, 0:N], b_ref[...])
+        q_ref[...] = prod[0:N]
+        f_ref[...] = prod[N:N + W]
+
+        @pl.when((step == 0) & (lax.axis_index("row") == 0))
+        def _():
+            keep = iota((W, 256), 1) < N
+            f_ref[:, 0:256] = jnp.where(keep, aux_ref[AUX_TOP:AUX_TOP + W, :], prod[N:N + W, 0:256])
+
+    @pl.when(careful)
+    def _():
+        q_ref[...] = b_ref[...]
+        copy = pltpu.make_async_copy(f_alt.at[:, pl.ds(pl.multiple_of(step * width, width), width)], f_ref, sem)
+        copy.start()
+        copy.wait()
+
+
+def products(b, f_alt, aux):
+    rows = b.shape[1]
+    width = rows // STEPS
+    out = lambda *shape: jax.ShapeDtypeStruct(shape, F32)
+    whole = pl.BlockSpec(memory_space=pltpu.VMEM)
+    return pl.pallas_call(
+        product_kernel,
+        name="products",
+        grid=(STEPS,),
+        out_shape=(out(N, rows), out(W, rows), out(NP, W), out(NP, W, W)),
+        in_specs=[pl.BlockSpec((N, width), lambda i: (0, i)), pl.BlockSpec(memory_space=pl.ANY), whole],
+        out_specs=(pl.BlockSpec((N, width), lambda i: (0, i)), pl.BlockSpec((W, width), lambda i: (0, i)), whole, whole),
+        scratch_shapes=[pltpu.SemaphoreType.DMA],
+        compiler_params=pltpu.CompilerParams(vmem_limit_bytes=32 * 1024 * 1024),
+    )(b, f_alt, aux)
+
+
+def all_pieces(x, axis, n):
+    me = lax.axis_index(axis)
+    got = jnp.stack([x] + [lax.ppermute(x, axis, [(i, (i + s) % n) for i in range(n)]) for s in range(1, n)])
+    return [lax.dynamic_index_in_dim(got, (me - j) % n, axis=0, keepdims=False) for j in range(n)]
+
+
+def ordered_sum(x, axis, n):
+    pieces = all_pieces(x, axis, n)
+    total = pieces[0]
+    for piece in pieces[1:]:
+        total = total + piece
+    return total
 
 
 def dot_high(lhs_mat, rhs_mat):
@@ -526,8 +587,8 @@
     return lax.fori_loop(0, panel_width, t_step, jnp.zeros((panel_width, panel_width), jnp.float32))
 
 
-def careful_program(proc_cols):
-    sum_rows = functools.partial(lax.psum, axis_name="row")
+def careful_program(proc_cols, proc_rows):
+    sum_rows = functools.partial(ordered_sum, axis="row", n=proc_rows)
 
     def local_program(a_loc):
         rows_loc, panels_loc, panel_width = a_loc.shape
@@ -544,7 +605,8 @@
             old_panel = lax.dynamic_index_in_dim(a_work, slot_idx, axis=1, keepdims=False)
             new_panel, refl_vecs, tau_vec = factor_panel(old_panel, row_start, panel_idx * panel_width, sum_rows)
             t_fac = build_tfac(refl_vecs, tau_vec, sum_rows)
-            refl_vecs, t_fac = lax.psum((jnp.where(is_owner, refl_vecs, 0.0), jnp.where(is_owner, t_fac, 0.0)), "col")
+            refl_vecs = ordered_sum(jnp.where(is_owner, refl_vecs, 0.0), "col", proc_cols)
+            t_fac = ordered_sum(jnp.where(is_owner, t_fac, 0.0), "col", proc_cols)
             a_work = lax.dynamic_update_index_in_dim(a_work, jnp.where(is_owner, new_panel, old_panel), slot_idx, axis=1)
             proj_sum = sum_rows(contract("rk,rsj->ksj", refl_vecs, a_work))
             w_block = contract("kl,ksj->lsj", t_fac, proj_sum)
@@ -568,7 +630,7 @@
             return q_local - contract("rk,ksj->rsj", refl_vecs, w_block)
 
         q_local = lax.fori_loop(0, num_panels, q_step, q_init)
-        gathered = lax.all_gather(q_local, "col")
+        gathered = jnp.stack(all_pieces(q_local, "col", proc_cols))
         q_rows = gathered.transpose(1, 2, 0, 3).reshape(rows_loc, num_panels * panel_width)
         tau_vals = jnp.diagonal(all_tfac, axis1=1, axis2=2)
         return a_work, tau_vals, all_tfac, q_rows
@@ -577,18 +639,19 @@
 
 
 def solution(mesh):
-    careful = careful_program(mesh.shape["col"])
+    careful = careful_program(mesh.shape["col"], mesh.shape["row"])
 
     def local_program(a_loc):
         rows_loc = a_loc.shape[0]
-        q_t, f_t, tau_vals, t_fac, flag = fused_qr(a_loc.reshape(rows_loc, W).T)
+        b, f_alt, aux, flag = gather_and_factor(a_loc.reshape(rows_loc, W).T)
 
         def again(state):
             factored, tau_new, t_new, q_new = careful(a_loc)
-            return jnp.float32(0.0), factored, tau_new, t_new, q_new
-
-        state = (flag[0, 0], f_t.T.reshape(rows_loc, 1, W), tau_vals, t_fac, q_t.T)
-        return lax.while_loop(lambda s: s[0] > 0.5, again, state)[1:]
+            return jnp.zeros((1,), F32), q_new.T, factored.reshape(rows_loc, W).T, pack_aux(tau_new, t_new)
+
+        b, f_alt, aux = lax.while_loop(lambda s: s[0][0] > 0.5, again, (flag, b, f_alt, aux))[1:]
+        q_t, f_t, tau_vals, t_fac = products(b, f_alt, aux)
+        return f_t.T.reshape(rows_loc, 1, W), tau_vals, t_fac, q_t.T
 
     spec_rows = P(("part", "row"), "col", None)
     out_specs = (spec_rows, P("part", None), P("part", None, None), P(("part", "row"), None))

time: 93.2 us -> 78.8 us (0.85)
  between operations: 14 us -> 0.81 us
  local copies, waits for them, and re-layouts: 10.1 us -> 0 us
  Pallas kernels: 67.9 us -> 76.8 us
    pallas_call x1 -> x2, Pallas kernels: 67.9 us -> 76.8 us  [the longest x1 67.7 us: gather_and_factor(): pl.pallas_call(gather_kernel, name='gather_and_factor', out_shape=(out(N,...]
    unnamed x4 -> x0, local copies, waits for them, and re-layouts: 8.85 us -> none
where the time goes in v2:
time: 78.8 us; the launch traced here: 78.5 us
  Pallas kernels  76.8 us (97%)
  loops' own time  0.81 us (1%)
  between operations  0.81 us (1%)
    pallas_call x1, Pallas kernels, gather_and_factor(): pl.pallas_call(gather_kernel, name='gather_and_factor', out_shape=(out(N,...  67.7 us
    pallas_call x1, Pallas kernels, products(): pl.pallas_call(product_kernel, name='products', grid=(STEPS,), out_shape=...  9.18 us

profile of v2, /device:TPU:0, one launch (start us, length us, event | category | flops | bytes accessed | tf_op | source)
XLA Modules:
  0.0 78.5 jit_solution(1257497207024785966)
XLA Ops:
  0.6 67.7 %gather_and_factor.1 = (f32[192,4096]{1,0:T(8,128)}, f32[48,4096]{1,0:T(8,128)}, f32[496,256]{1,0:T(8,128)}, f32[1]{0:T(128)}) custom-call(f32[48,4096]{1,0:T(8,128)} %bitcast.291), custom_call_target="tpu_custom_call" | custom-call | tf_op jit(solution)/shard_map/gather_and_factor/pallas_call | solution.py:447
  68.3 0.8 %while.136 = (f32[1]{0:T(128)}, f32[192,4096]{1,0:T(8,128)}, f32[48,4096]{1,0:T(8,128)}, f32[496,256]{1,0:T(8,128)}, f32[4096,1,48]{0,2,1:T(8,128)}) while((f32[1]{0:T(128)}, f32[192,4096]{1,0:T(8,128)}, f32[48,4096]{1,0:T(8,128)}, f32[496,256]{1,0:T(8,128)}, f32[4096,1,48]{0,2,1:T(8,128)}) %tuple.213), condition=%region_9.10_spmd, body=%region_0.9_spmd | while | flops 581720192 | bytes 76352696 | solution.py:652
  69.1 9.2 %products.1 = (f32[192,4096]{1,0:T(8,128)}, f32[48,4096]{1,0:T(8,128)}, f32[4,48]{1,0:T(4,128)}, f32[4,48,48]{2,1,0:T(8,128)}) custom-call(f32[192,4096]{1,0:T(8,128)} %get-tuple-element.725.b_ref, f32[48,4096]{1,0:T(8,128)} %get-tuple-element.726.f_alt, f32[496,256]{1,0:T(8,128)} %get-tuple-element.727.aux_ref), custom_call_target="tpu_custom_call" | custom-call | tf_op jit(solution)/shard_map/products/pallas_call | solution.py:505

commit v3 on v2

--- a/solution.py
+++ b/solution.py
@@ -12,10 +12,11 @@
 NP = 4
 N = W * NP
 NC = 8
-WIN = 4
+WIN = 6
 F32 = jnp.float32
 SUM_BOUND = 6144.0
-STEPS = 8
+HEAD0, HEAD1, HEAD2 = 3, 5, 2
+STEPS = 2
 AUX_TOP = N + W
 AUX_T = AUX_TOP + W
 AUX_TAU = AUX_T + N
@@ -44,7 +45,7 @@
     return jnp.concatenate([x, jnp.zeros((x.shape[0], lanes - x.shape[1]), F32)], axis=1)
 
 
-def chain(limit, xc_ref, hn_ref, vt_ref, fr_ref, rn_ref, td_ref):
+def chain(limit, xc_ref, hn_ref, vt_ref, fr_ref, rn_ref, td_ref, zt_ref):
     ng = W // 8
     sub = iota((8, 128), 0)
     lane = iota((8, 128), 1)
@@ -53,6 +54,7 @@
     xs0 = [xc_ref[8 * s:8 * s + 8, 0:128] for s in range(ng)]
     xs1 = [xc_ref[8 * s:8 * s + 8, 128:256] for s in range(ng)]
     hs = [hn_ref[8 * s:8 * s + 8, :] for s in range(ng)]
+    zs = [jnp.where(lane == sub + 8 * s, 1.0, 0.0) for s in range(ng)]
 
     def bcast_sub(x, u):
         return jnp.broadcast_to(x[u:u + 1, :], (8, 128))
@@ -61,12 +63,13 @@
         return jnp.broadcast_to(x[:, k:k + 1], (8, 128))
 
     def columns(k):
-        return ({s: bcast_col(hs[s], k) for s in range(k // 8, ng)}, {s: bcast_col(xs0[s], k) for s in range(0, ng)})
+        return ({s: bcast_col(hs[s], k) for s in range(k // 8, ng)}, {s: bcast_col(xs0[s], k) for s in range(0, ng)},
+                {s: bcast_col(zs[s], k) for s in range(k // 8 + 1)})
 
     window = {k: columns(k) for k in range(WIN)}
     for k in range(W):
         s0, u = k // 8, k % 8
-        ch, cx = window.pop(k)
+        ch, cx, cz = window.pop(k)
         hkk = bcast_sub(ch[s0], u)
         alpha = bcast_sub(cx[s0], u)
         inv_norm = lax.rsqrt(hkk)
@@ -83,13 +86,15 @@
             wc[s] = jnp.where(below, w, 0.0) if s == s0 else w
         r_of = {}
         for m in range(k + 1, min(k + WIN, W)):
-            mh, mx = window[m]
+            mh, mx, mz = window[m]
             r_m = bcast_sub(rc[m // 8], m % 8)
             v_m = bcast_sub(mx[s0], u) * inv
             for s in range(m // 8, ng):
                 mh[s] = mh[s] - rc[s] * r_m
             for s in range(s0, ng):
                 mx[s] = mx[s] - wc[s] * v_m
+            for s in range(s0 + 1):
+                mz[s] = mz[s] - cz[s] * v_m
         hrow = bcast_sub(hs[s0], u) * inv_beta
         x0 = bcast_sub(xs0[s0], u)
         x1 = bcast_sub(xs1[s0], u)
@@ -106,13 +111,18 @@
             hs[s] = hs[s] - rc[s] * hrow
             xs0[s] = xs0[s] - wc[s] * v0
             xs1[s] = xs1[s] - wc[s] * v1
+        v_next = jnp.where(lane == k, 0.0, v0)
+        for s in range(s0 + 1):
+            zs[s] = zs[s] - cz[s] * v_next
         if k + WIN < W:
             window[k + WIN] = columns(k + WIN)
+    for s in range(ng):
+        zt_ref[8 * s:8 * s + 8, :] = zs[s]
 
 
 def load_panel(g, refs):
-    xt, e1, e2, rts, wts, rinvd, rnat, kvt, xc_ref, hn_ref, dvec = (
-        refs["xt"], refs["e1"], refs["e2"], refs["rts"], refs["wts"], refs["rinvd"], refs["rnat"], refs["kv"], refs["xc"], refs["hn"], refs["dvec"])
+    xt, e1, e2, rts, wts, rinvd, kvt, xc_ref, hn_ref, dvec = (
+        refs["xt"], refs["e1"], refs["e2"], refs["rts"], refs["wts"], refs["rinvd"], refs["kv"], refs["xc"], refs["hn"], refs["dvec"])
     x = xt[g]
     lane = iota((W, 256), 1)
     row = iota((W, 256), 0)
@@ -133,8 +143,7 @@
         for q in range(h):
             hgh = hgh - mm_nt(rts[g, q], rts[h, q])
         rt = mm_nt(hgh, rinvd[h])
-        d = hgh - mm(x[:, 0:W], rnat[h])
-        both = mm(d, kvt[h])
+        both = mm(x[:, 0:W] - rt, kvt[h])
         x = roll(x - both[:, 0:256], 256 - W)
         hgg = hgg - mm_nt(rt, rt)
         rts[g, h] = rt
@@ -160,21 +169,17 @@
     rinvt = roll(rn, 64)[:, 0:W]
     rinvt = jnp.where(sq_lane <= sq_row, rinvt, 0.0)
     mt = jnp.where(sq_lane <= sq_row, mt, 0.0)
+    refs["rinvd"][g] = rinvt
     refs["rnat"][g] = rnat
-    refs["rinvd"][g] = rinvt
-    s = -mm(v[:, 0:W], mm_nt(rnat, mt))
-    t = td[:, 0:W]
+    refs["mts"][g] = mt
+    refs["v1"][g] = v[:, 0:W]
+    refs["t"][g] = td[:, 0:W]
     refs["tau"][g:g + 1, :] = jnp.sum(td, axis=0, keepdims=True)[:, 0:W]
-    size = 1
-    while size < W:
-        pair = (sq_row // (2 * size) == sq_lane // (2 * size)) & (sq_row // size < sq_lane // size)
-        t = t - mm(mm(t, jnp.where(pair, s, 0.0)), t)
-        size *= 2
-    refs["t"][g] = t
+    zt = refs["zt"][:, 0:W]
+    refs["zsum"][...] = refs["zsum"][...] + jnp.sum(zt * zt)
     if g + 1 < NP:
-        kmat = lax.dot_general(mt, t, (((0,), (0,)), ((), ())), precision=HIGHEST, preferred_element_type=F32)
-        refs["kv"][g, :, 0:256] = mm(kmat, v)
-        refs["kv"][g, :, 256:384] = widen(kmat, 128)
+        refs["kv"][g, :, 0:256] = mm(zt, v)
+        refs["kv"][g, :, 256:384] = widen(zt, 128)
     lr = roll(widen(rinvt, 256), W * g)
     lc = roll(widen(mt, 256), W * g)
     if g:
@@ -186,11 +191,27 @@
     refs["lc"][W * g:W * g + W, :] = lc
 
 
+def build_t(refs):
+    sq_lane = iota((W, W), 1)
+    sq_row = iota((W, W), 0)
+    prods = [mm_nt(refs["rnat"][g], refs["mts"][g]) for g in range(NP)]
+    ss = [-mm(refs["v1"][g], prods[g]) for g in range(NP)]
+    ts = [refs["t"][g] for g in range(NP)]
+    size = 1
+    while size < W:
+        pair = (sq_row // (2 * size) == sq_lane // (2 * size)) & (sq_row // size < sq_lane // size)
+        halves = [mm(ts[g], jnp.where(pair, ss[g], 0.0)) for g in range(NP)]
+        ts = [ts[g] - mm(halves[g], ts[g]) for g in range(NP)]
+        size *= 2
+    for g in range(NP):
+        refs["t"][g] = ts[g]
+
+
 def gather_kernel(a_hbm, b_hbm, f_alt, aux_ref, flag_ref, panels, xt, e1, e2, x0s, x1s, x2s, x3s, g1s, g1r, g2s, g2r, h1s, h1r, h2s, h2r,
-                 rts, wts, rinvd, rnat, kvt, xc, hn, dvec, vt, fr, rn, td, ftop, lr, lc, tau, t_fac, bad_mine, bad_other,
-                 load_sem, send_sem, bulk_sem, ex_send, ex_recv, e0_send, e0_recv, e1_send, e1_recv, e2_send, e2_recv, flag_sem, write_sem):
+                 rts, wts, rinvd, rnat, kvt, xc, hn, dvec, vt, fr, rn, td, ftop, lr, lc, tau, t_fac, zt, mts, v1s, zsum, bad_mine, bad_other,
+                 load_sem, send_sem, bulk_sem, ex_send, ex_recv, e0_send, e0_recv, e0_row, e1_send, e1_recv, e1_row, e2_send, e2_recv, e2_row, flag_sem, write_sem):
     refs = dict(xt=xt, e1=e1, e2=e2, rts=rts, wts=wts, rinvd=rinvd, rnat=rnat, kv=kvt, xc=xc, hn=hn, dvec=dvec,
-                vt=vt, fr=fr, rn=rn, td=td, ftop=ftop, lr=lr, lc=lc, tau=tau, t=t_fac)
+                vt=vt, fr=fr, rn=rn, td=td, ftop=ftop, lr=lr, lc=lc, tau=tau, t=t_fac, zt=zt, mts=mts, v1=v1s, zsum=zsum)
     part = lax.axis_index("part")
     c = lax.axis_index("col")
     r = lax.axis_index("row")
@@ -205,18 +226,18 @@
         pltpu.make_async_copy(a_hbm.at[:, pl.ds(q * width, width)], panels.at[c, q], load_sem.at[q]).start()
 
     barrier = pltpu.get_barrier_semaphore()
-    for s in range(1, NP):
-        pl.semaphore_signal(barrier, inc=1, device_id=at(lax.rem(c + s, NP), r), device_id_type=MESH)
-    pl.semaphore_signal(barrier, inc=1, device_id=at(c, twin), device_id_type=MESH)
-    pl.semaphore_signal(barrier, inc=1, device_id=at(c, across), device_id_type=MESH)
-    pl.semaphore_signal(barrier, inc=1, device_id=(1 - part, c, r), device_id_type=MESH)
-    pl.semaphore_wait(barrier, NP + 2)
+    peers = [at(lax.rem(c + s, NP), r) for s in range(1, NP)] + [at(c, twin), at(c, across), (1 - part, c, r)]
+    for peer in peers:
+        pl.semaphore_signal(barrier, inc=1, device_id=peer, device_id_type=MESH)
+    pl.semaphore_wait(barrier, len(peers))
 
     lr[...] = jnp.zeros_like(lr)
     lc[...] = jnp.zeros_like(lc)
     dvec[...] = jnp.zeros_like(dvec)
+    zsum[...] = jnp.zeros_like(zsum)
     e2[...] = jnp.zeros_like(e2)
 
+    order_load = [q for i in range(NC // 2) for q in (i, i + NC // 2)]
     order_l = list(range(NC))
     order_r = list(range(NC // 2, NC)) + list(range(NC // 2))
 
@@ -268,77 +289,119 @@
         second.wait()
         out[slot] = half[...] + got2[...]
 
-    def shared(ref, slot, ssem, rsem, sslot, s, rslot):
-        return pltpu.make_async_remote_copy(ref.at[slot], ref.at[slot], ssem.at[sslot], rsem.at[rslot],
-                                            device_id=at(lax.rem(c + s, NP), r), device_id_type=MESH)
+    rows_mine = pl.ds(pl.multiple_of(lax.rem(r, 2) * (W // 2), 8), W // 2)
+    lanes_mine = pl.ds(pl.multiple_of(lax.div(r, 2) * 128, 128), 128)
+
+    class Message:
+        def __init__(self, ref, slot, sems, quarter, source):
+            self.ref, self.slot, self.sems, self.quarter, self.source = ref, slot, sems, quarter, source
+
+        def copy(self, ref, send, recv, peer):
+            return pltpu.make_async_remote_copy(ref, ref, send, recv, device_id=peer, device_id_type=MESH)
+
+        def hop(self, s):
+            part_ref = self.ref.at[self.slot, rows_mine, lanes_mine] if self.quarter else self.ref.at[self.slot, rows_mine]
+            return self.copy(part_ref, self.sems[0].at[s - 1, self.slot], self.sems[1].at[self.slot], at(lax.rem(c + s, NP), r))
+
+        def to_twin(self):
+            part_ref = self.ref.at[self.slot, rows_mine, lanes_mine] if self.quarter else self.ref.at[self.slot, rows_mine]
+            return self.copy(part_ref, self.sems[2].at[0, self.slot], self.sems[2].at[1, self.slot], at(c, twin))
+
+        def to_across(self):
+            return self.copy(self.ref.at[self.slot, :, lanes_mine], self.sems[2].at[2, self.slot], self.sems[2].at[3, self.slot], at(c, across))
+
+        def each_hop(self, act):
+            @pl.when(c == self.source)
+            def _():
+                for s in range(1, NP):
+                    act(self.hop(s))
+
+        def send_on(self):
+            self.each_hop(lambda cp: cp.start())
+
+        def receive(self):
+            @pl.when(c != self.source)
+            def _():
+                self.hop(1).wait_recv()
+                self.to_twin().start()
+
+        def join(self):
+            @pl.when(c != self.source)
+            def _():
+                self.to_twin().wait()
+                if self.quarter:
+                    self.to_across().start()
+
+        def finish(self):
+            if self.quarter:
+                @pl.when(c != self.source)
+                def _():
+                    self.to_across().wait()
+
+    msg0 = [Message(xt, g, (e0_send, e0_recv, e0_row), True, g) for g in range(NP)]
+    msg1 = [None] + [Message(e1, g, (e1_send, e1_recv, e1_row), False, g - 1) for g in range(1, NP)]
+    msg2 = [Message(e2, i, (e2_send, e2_recv, e2_row), False, i + 1) for i in range(2)]
+
+    def take(messages):
+        for m in messages:
+            m.receive()
+        for m in messages:
+            m.join()
+        for m in messages:
+            m.finish()
 
     def chunk_cols(g, q):
         return panels[g, q]
 
+    started = 0
     for q in range(NC):
-        pltpu.make_async_copy(a_hbm.at[:, pl.ds(q * width, width)], panels.at[c, q], load_sem.at[q]).wait()
-    head = 3
-    for i in range(head):
-        start_own(i)
-    for q in range(NC):
-        write(c, q).start()
+        pltpu.make_async_copy(a_hbm.at[:, pl.ds(order_load[q] * width, width)], panels.at[c, order_load[q]], load_sem.at[order_load[q]]).wait()
+        if q % 2 and started < HEAD0:
+            start_own(started)
+            started += 1
     gram = jnp.zeros((W, W), F32)
     for q in range(NC):
         blk = chunk_cols(c, q)
         gram = gram + mm_nt(blk, blk)
+    for q in range(NC):
+        write(c, q).start()
     lane = iota((W, 256), 1)
     top = jnp.where((lane < N) & (r == 0), panels[c, 0, :, 0:256], 0.0)
     x0s[...] = top + roll(widen(gram, 256), N)
     row_sum(0, x0s, x1s, x2s, x3s, xt, c)
-    for s in range(1, NP):
-        shared(xt, c, e0_send, e0_recv, s - 1, s, c).start()
-    for i in range(head, NC):
+    for m in msg0:
+        m.send_on()
+    for i in range(started, NC):
         start_own(i)
-
-    def wait_e0(g):
-        @pl.when(c != g)
-        def _():
-            shared(xt, g, e0_send, e0_recv, 0, 1, g).wait_recv()
-
-    def wait_e1(g):
-        @pl.when(c != g - 1)
-        def _():
-            shared(e1, g, e1_send, e1_recv, 0, 1, g).wait_recv()
-
-    def wait_e2(i):
-        @pl.when(c != i + 1)
-        def _():
-            shared(e2, i, e2_send, e2_recv, 0, 1, i).wait_recv()
 
     def before(g):
         if g == 0:
-            wait_e0(0)
+            take(msg0)
         if g == 1:
+            g1s[...] = jnp.zeros_like(g1s)
+            left = jnp.maximum(c - 1, 0)
             for i in range(NC):
                 arrive(1, i)
-                if i < head:
+                if i < HEAD1:
                     forward(1, i)
+
+                @pl.when(c <= NP - 2)
+                def _():
+                    for q in ([i, i - NC // 2] if i >= NC // 2 else []):
+                        pair = jnp.concatenate([chunk_cols(c, q), chunk_cols(left, q)], axis=0)
+                        g1s[:, 0:2 * W] += mm_nt(chunk_cols(c + 1, q), pair)
 
             @pl.when(c <= NP - 2)
             def _():
-                left = jnp.maximum(c - 1, 0)
-                acc = jnp.zeros((W, 2 * W), F32)
-                for q in range(NC):
-                    pair = jnp.concatenate([chunk_cols(c, q), chunk_cols(left, q)], axis=0)
-                    acc = acc + mm_nt(chunk_cols(c + 1, q), pair)
-                g1s[...] = widen(acc, 128)
                 row_sum(1, g1s, g1r, g2s, g2r, e1, c + 1)
-                for s in range(1, NP):
-                    shared(e1, c + 1, e1_send, e1_recv, s - 1, s, c + 1).start()
-            for i in range(head, NC):
+            for m in msg1[1:]:
+                m.send_on()
+            for i in range(HEAD1, NC):
                 forward(1, i)
-            wait_e0(1)
-            wait_e1(1)
-        if g == 2:
             half = NC // 2
             for i in range(half):
                 arrive(2, i)
-                if i < 1:
+                if i < HEAD2:
                     forward(2, i)
 
             @pl.when((c >= 1) & (c <= 2))
@@ -349,20 +412,17 @@
                     acc = acc + mm_nt(chunk_cols(3, base + i), chunk_cols(0, base + i))
                 h1s[...] = widen(acc, 128)
                 row_sum(2, h1s, h1r, h2s, h2r, e2, c - 1)
-                for s in range(1, NP):
-                    shared(e2, c - 1, e2_send, e2_recv, s - 1, s, c - 1).start()
-            for i in range(1, half):
+            for m in msg2:
+                m.send_on()
+            for i in range(HEAD2, half):
                 forward(2, i)
-            wait_e0(2)
-            wait_e1(2)
-        if g == 3:
+            take(msg1[1:])
+        if g == 2:
             for i in range(NC // 2, NC):
                 arrive(2, i)
                 forward(2, i)
-            wait_e0(3)
-            wait_e1(3)
-            wait_e2(0)
-            wait_e2(1)
+        if g == 3:
+            take(msg2)
 
     def panel_step(g, carry):
         for s in range(NP):
@@ -370,7 +430,7 @@
             def _():
                 before(s)
                 load_panel(s, refs)
-        chain(256 - W * g, xc, hn, vt, fr, rn, td)
+        chain(256 - W * g, xc, hn, vt, fr, rn, td, zt)
         for s in range(NP):
             @pl.when(g == s)
             def _():
@@ -383,10 +443,11 @@
     lr_all = lr[...][:, 0:N]
     lc_all = lc[...][:, 0:N]
     good = ((jnp.sum(lr_all * lr_all * dv) <= SUM_BOUND) & (jnp.sum(lc_all * lc_all * dv) <= SUM_BOUND)
-            & (jnp.min(dv) > 1e-18) & (jnp.max(dv) < 1e30))
+            & (jnp.max(zsum[...]) <= SUM_BOUND) & (jnp.min(dv) > 1e-18) & (jnp.max(dv) < 1e30))
     bad_mine[...] = jnp.zeros((8, 128), F32) + jnp.where(good, 0.0, 1.0)
     flag_copy = pltpu.make_async_remote_copy(bad_mine, bad_other, flag_sem.at[0], flag_sem.at[1], device_id=(1 - part, c, r), device_id_type=MESH)
     flag_copy.start()
+    build_t(refs)
 
     aux_ref[0:N, :] = lr[...]
     aux_ref[N:N + W, :] = lc[pl.ds(pl.multiple_of(c * W, W), W), :]
@@ -418,16 +479,8 @@
                 @pl.when(c >= s)
                 def _():
                     bulk(1, s, i).wait_send()
-    for s in range(1, NP):
-        shared(xt, c, e0_send, e0_recv, s - 1, s, c).wait_send()
-
-        @pl.when(c <= NP - 2)
-        def _():
-            shared(e1, c + 1, e1_send, e1_recv, s - 1, s, c + 1).wait_send()
-
-        @pl.when((c >= 1) & (c <= 2))
-        def _():
-            shared(e2, c - 1, e2_send, e2_recv, s - 1, s, c - 1).wait_send()
+    for m in msg0 + msg1[1:] + msg2:
+        m.each_hop(lambda cp: cp.wait_send())
 
 
 def gather_and_factor(a_t):
@@ -442,8 +495,9 @@
     scratch += [vm(W, 128)] * 8
     scratch += [vm(NP, 3, W, W), vm(NP, 3, W, W), vm(NP, W, W), vm(NP, W, W), vm(3, W, 384), vm(W, 256), vm(W, 128), vm(8, 256),
                 vm(W, 256), vm(W, 256), vm(W, 128), vm(W, 128), vm(NP, W, 256), vm(N, 256), vm(N, 256),
-                vm(NP, W), vm(NP, W, W), vm(8, 128), vm(8, 128)]
-    scratch += [dma(NC), dma(2, NP, NC), dma(NP, NC), dma(3, 2), dma(3, 2), dma(3), dma(NP), dma(3), dma(NP), dma(3), dma(2), dma(2), dma(NP, NC)]
+                vm(NP, W), vm(NP, W, W), vm(W, 128), vm(NP, W, W), vm(NP, W, W), vm(8, 128), vm(8, 128), vm(8, 128)]
+    scratch += [dma(NC), dma(2, NP, NC), dma(NP, NC), dma(3, 2), dma(3, 2), dma(3, NP), dma(NP), dma(4, NP), dma(3, NP), dma(NP), dma(4, NP),
+                dma(3, 2), dma(2), dma(4, 2), dma(2), dma(NP, NC)]
     return pl.pallas_call(
         gather_kernel,
         name="gather_and_factor",

time: 78.8 us -> 70.5 us (0.89)
  Pallas kernels: 76.8 us -> 68.7 us
    pallas_call x1, Pallas kernels: 67.7 us -> 62.1 us  [gather_and_factor(): pl.pallas_call(gather_kernel, name='gather_and_factor', out_shape=(out(N,...]
    pallas_call x1, Pallas kernels: 9.18 us -> 6.57 us  [products(): pl.pallas_call(product_kernel, name='products', grid=(STEPS,), out_shape=...]
where the time goes in v3:
time: 70.5 us; the launch traced here: 70.3 us
  Pallas kernels  68.7 us (97%)
  loops' own time  0.81 us (1%)
  between operations  0.81 us (1%)
    pallas_call x1, Pallas kernels, gather_and_factor(): pl.pallas_call(gather_kernel, name='gather_and_factor', out_shape=(out(N,...  62.1 us
    pallas_call x1, Pallas kernels, products(): pl.pallas_call(product_kernel, name='products', grid=(STEPS,), out_shape=...  6.57 us

profile of v3, /device:TPU:0, one launch (start us, length us, event | category | flops | bytes accessed | tf_op | source)
XLA Modules:
  0.0 70.3 jit_solution(11279567572919374169)
XLA Ops:
  0.6 62.1 %gather_and_factor.1 = (f32[192,4096]{1,0:T(8,128)}, f32[48,4096]{1,0:T(8,128)}, f32[496,256]{1,0:T(8,128)}, f32[1]{0:T(128)}) custom-call(f32[48,4096]{1,0:T(8,128)} %bitcast.291), custom_call_target="tpu_custom_call" | custom-call | tf_op jit(solution)/shard_map/gather_and_factor/pallas_call | solution.py:501
  62.8 0.8 %while.136 = (f32[1]{0:T(128)}, f32[192,4096]{1,0:T(8,128)}, f32[48,4096]{1,0:T(8,128)}, f32[496,256]{1,0:T(8,128)}, f32[4096,1,48]{0,2,1:T(8,128)}) while((f32[1]{0:T(128)}, f32[192,4096]{1,0:T(8,128)}, f32[48,4096]{1,0:T(8,128)}, f32[496,256]{1,0:T(8,128)}, f32[4096,1,48]{0,2,1:T(8,128)}) %tuple.213), condition=%region_9.10_spmd, body=%region_0.9_spmd | while | flops 581720192 | bytes 76352696 | solution.py:706
  63.6 6.6 %products.1 = (f32[192,4096]{1,0:T(8,128)}, f32[48,4096]{1,0:T(8,128)}, f32[4,48]{1,0:T(4,128)}, f32[4,48,48]{2,1,0:T(8,128)}) custom-call(f32[192,4096]{1,0:T(8,128)} %get-tuple-element.725.b_ref, f32[48,4096]{1,0:T(8,128)} %get-tuple-element.726.f_alt, f32[496,256]{1,0:T(8,128)} %get-tuple-element.727.aux_ref), custom_call_target="tpu_custom_call" | custom-call | tf_op jit(solution)/shard_map/products/pallas_call | solution.py:559

commit v4 on v3

--- a/solution.py
+++ b/solution.py
@@ -16,12 +16,11 @@
 F32 = jnp.float32
 SUM_BOUND = 6144.0
 HEAD0, HEAD1, HEAD2 = 3, 5, 2
-STEPS = 2
-AUX_TOP = N + W
-AUX_T = AUX_TOP + W
+STEPS = 4
+EARLY = NC - NC // STEPS
+AUX_T = N + W
 AUX_TAU = AUX_T + N
-AUX_MODE = AUX_TAU + 8
-AUX_ROWS = AUX_MODE + 8
+AUX_ROWS = AUX_TAU + 8
 
 
 def mm(a, b):
@@ -207,9 +206,9 @@
         refs["t"][g] = ts[g]
 
 
-def gather_kernel(a_hbm, b_hbm, f_alt, aux_ref, flag_ref, panels, xt, e1, e2, x0s, x1s, x2s, x3s, g1s, g1r, g2s, g2r, h1s, h1r, h2s, h2r,
+def gather_kernel(a_hbm, b_ref, f_alt, aux_ref, flag_ref, panels, xt, e1, e2, x0s, x1s, x2s, x3s, g1s, g1r, g2s, g2r, h1s, h1r, h2s, h2r,
                  rts, wts, rinvd, rnat, kvt, xc, hn, dvec, vt, fr, rn, td, ftop, lr, lc, tau, t_fac, zt, mts, v1s, zsum, bad_mine, bad_other,
-                 load_sem, send_sem, bulk_sem, ex_send, ex_recv, e0_send, e0_recv, e0_row, e1_send, e1_recv, e1_row, e2_send, e2_recv, e2_row, flag_sem, write_sem):
+                 load_sem, send_sem, bulk_sem, ex_send, ex_recv, e0_send, e0_recv, e0_row, e1_send, e1_recv, e1_row, e2_send, e2_recv, e2_row, flag_sem):
     refs = dict(xt=xt, e1=e1, e2=e2, rts=rts, wts=wts, rinvd=rinvd, rnat=rnat, kv=kvt, xc=xc, hn=hn, dvec=dvec,
                 vt=vt, fr=fr, rn=rn, td=td, ftop=ftop, lr=lr, lc=lc, tau=tau, t=t_fac, zt=zt, mts=mts, v1=v1s, zsum=zsum)
     part = lax.axis_index("part")
@@ -256,19 +255,14 @@
         def _():
             bulk(1, c, order_r[i]).start()
 
-    def write(g, q):
-        return pltpu.make_async_copy(panels.at[g, q], b_hbm.at[pl.ds(pl.multiple_of(g * W, W), W), pl.ds(q * width, width)], write_sem.at[g, q])
-
     def arrive(dist, i):
         @pl.when(c + dist <= NP - 1)
         def _():
             bulk(0, c + dist, order_l[i]).wait_recv()
-            write(c + dist, order_l[i]).start()
 
         @pl.when(c - dist >= 0)
         def _():
             bulk(1, c - dist, order_r[i]).wait_recv()
-            write(c - dist, order_r[i]).start()
 
     def forward(dist, i):
         @pl.when((c + dist <= NP - 1) & (c >= 1))
@@ -363,8 +357,6 @@
     for q in range(NC):
         blk = chunk_cols(c, q)
         gram = gram + mm_nt(blk, blk)
-    for q in range(NC):
-        write(c, q).start()
     lane = iota((W, 256), 1)
     top = jnp.where((lane < N) & (r == 0), panels[c, 0, :, 0:256], 0.0)
     x0s[...] = top + roll(widen(gram, 256), N)
@@ -451,19 +443,29 @@
 
     aux_ref[0:N, :] = lr[...]
     aux_ref[N:N + W, :] = lc[pl.ds(pl.multiple_of(c * W, W), W), :]
-    aux_ref[AUX_TOP:AUX_TOP + W, :] = ftop[c]
     for g in range(NP):
         aux_ref[AUX_T + W * g:AUX_T + W * g + W, :] = widen(t_fac[g], 256)
     aux_ref[AUX_TAU:AUX_TAU + 8, :] = jnp.concatenate([widen(tau[...], 256), jnp.zeros((4, 256), F32)], axis=0)
-    aux_ref[AUX_MODE:AUX_MODE + 8, :] = jnp.zeros((8, 256), F32)
-
+
+    ftop_c = ftop[c]
     for i in range(NC):
         arrive(3, i)
+        q = lax.rem(i + jnp.where(c >= NP // 2, NC // 2, 0), NC)
+        cols = pl.ds(pl.multiple_of(q * width, width), width)
+        if i < EARLY:
+            prod = mm(aux_ref[0:N + W, 0:N], jnp.concatenate([panels[g, q] for g in range(NP)], axis=0))
+            b_ref[:, cols] = prod[0:N]
+            f_alt[:, cols] = prod[N:N + W]
+
+            @pl.when((q == 0) & (r == 0))
+            def _():
+                keep = iota((W, 256), 1) < N
+                f_alt[:, 0:256] = jnp.where(keep, ftop_c, prod[N:N + W, 0:256])
+        else:
+            for g in range(NP):
+                b_ref[g * W:g * W + W, cols] = panels[g, q]
     flag_copy.wait()
     flag_ref[0] = jnp.max(jnp.maximum(bad_mine[...], bad_other[...]))
-    for g in range(NP):
-        for q in range(NC):
-            write(g, q).wait()
 
     for i in range(NC):
         @pl.when(c >= 1)
@@ -490,6 +492,7 @@
     dma = lambda *shape: pltpu.SemaphoreType.DMA(shape)
     out = lambda *shape: jax.ShapeDtypeStruct(shape, F32)
     hbm = pl.BlockSpec(memory_space=pl.ANY)
+    vmem = pl.BlockSpec(memory_space=pltpu.VMEM)
     scratch = [vm(NP, NC, W, width), vm(NP, W, 256), vm(NP, W, 128), vm(2, W, 128), vm(W, 256), vm(W, 256), vm(W, 256)]
     scratch += [vm(W, 256)]
     scratch += [vm(W, 128)] * 8
@@ -497,58 +500,50 @@
                 vm(W, 256), vm(W, 256), vm(W, 128), vm(W, 128), vm(NP, W, 256), vm(N, 256), vm(N, 256),
                 vm(NP, W), vm(NP, W, W), vm(W, 128), vm(NP, W, W), vm(NP, W, W), vm(8, 128), vm(8, 128), vm(8, 128)]
     scratch += [dma(NC), dma(2, NP, NC), dma(NP, NC), dma(3, 2), dma(3, 2), dma(3, NP), dma(NP), dma(4, NP), dma(3, NP), dma(NP), dma(4, NP),
-                dma(3, 2), dma(2), dma(4, 2), dma(2), dma(NP, NC)]
+                dma(3, 2), dma(2), dma(4, 2), dma(2)]
     return pl.pallas_call(
         gather_kernel,
         name="gather_and_factor",
         out_shape=(out(N, rows), out(W, rows), out(AUX_ROWS, 256), out(1)),
         in_specs=[hbm],
-        out_specs=(hbm, hbm, pl.BlockSpec(memory_space=pltpu.VMEM), pl.BlockSpec(memory_space=pltpu.SMEM)),
+        out_specs=(vmem, vmem, vmem, pl.BlockSpec(memory_space=pltpu.SMEM)),
         scratch_shapes=scratch,
         compiler_params=pltpu.CompilerParams(collective_id=0, has_side_effects=True, vmem_limit_bytes=32 * 1024 * 1024),
     )(a_t)
 
 
-def pack_kernel(tau_ref, t_ref, aux_ref):
-    aux_ref[...] = jnp.zeros_like(aux_ref)
+def product_kernel(b_ref, f_alt, aux_ref, q_hbm, f_hbm, tau_ref, t_ref, q_late, f_late, sems):
+    width = q_late.shape[1]
+
+    def out(block, q_src, f_src):
+        cols = pl.ds(pl.multiple_of(block * width, width), width)
+        return (pltpu.make_async_copy(q_src, q_hbm.at[:, cols], sems.at[0, block]),
+                pltpu.make_async_copy(f_src, f_hbm.at[:, cols], sems.at[1, block]))
+
+    late = jnp.where(lax.axis_index("col") >= NP // 2, STEPS // 2 - 1, STEPS - 1)
+
+    def each_early(act):
+        for i in range(1, STEPS):
+            block = lax.rem(late + i, STEPS)
+            cols = pl.ds(pl.multiple_of(block * width, width), width)
+            for cp in out(block, b_ref.at[:, cols], f_alt.at[:, cols]):
+                act(cp)
+
+    each_early(lambda cp: cp.start())
+    tau_ref[...] = aux_ref[AUX_TAU:AUX_TAU + NP, 0:W]
     for g in range(NP):
-        aux_ref[AUX_T + W * g:AUX_T + W * g + W, 0:W] = t_ref[g]
-    aux_ref[AUX_TAU:AUX_TAU + NP, 0:W] = tau_ref[...]
-    aux_ref[AUX_MODE:AUX_MODE + 8, :] = jnp.ones((8, 256), F32)
-
-
-def pack_aux(tau_vals, t_fac):
-    return pl.pallas_call(pack_kernel, name="pack_aux", out_shape=jax.ShapeDtypeStruct((AUX_ROWS, 256), F32))(tau_vals, t_fac)
-
-
-def product_kernel(b_ref, f_alt, aux_ref, q_ref, f_ref, tau_ref, t_ref, sem):
-    step = pl.program_id(0)
-    width = b_ref.shape[1]
-    careful = jnp.max(aux_ref[AUX_MODE:AUX_MODE + 8, 0:128]) > 0.5
-
-    @pl.when(step == 0)
-    def _():
-        tau_ref[...] = aux_ref[AUX_TAU:AUX_TAU + NP, 0:W]
-        for g in range(NP):
-            t_ref[g] = aux_ref[AUX_T + W * g:AUX_T + W * g + W, 0:W]
-
-    @pl.when(jnp.logical_not(careful))
-    def _():
-        prod = mm(aux_ref[0:N + W, 0:N], b_ref[...])
-        q_ref[...] = prod[0:N]
-        f_ref[...] = prod[N:N + W]
-
-        @pl.when((step == 0) & (lax.axis_index("row") == 0))
-        def _():
-            keep = iota((W, 256), 1) < N
-            f_ref[:, 0:256] = jnp.where(keep, aux_ref[AUX_TOP:AUX_TOP + W, :], prod[N:N + W, 0:256])
-
-    @pl.when(careful)
-    def _():
-        q_ref[...] = b_ref[...]
-        copy = pltpu.make_async_copy(f_alt.at[:, pl.ds(pl.multiple_of(step * width, width), width)], f_ref, sem)
-        copy.start()
-        copy.wait()
+        t_ref[g] = aux_ref[AUX_T + W * g:AUX_T + W * g + W, 0:W]
+    half = width // 2
+    for i in range(2):
+        prod = mm(aux_ref[0:N + W, 0:N], b_ref[:, pl.ds(pl.multiple_of(late * width + i * half, half), half)])
+        q_late[:, i * half:i * half + half] = prod[0:N]
+        f_late[:, i * half:i * half + half] = prod[N:N + W]
+    last = out(late, q_late, f_late)
+    for cp in last:
+        cp.start()
+    each_early(lambda cp: cp.wait())
+    for cp in last:
+        cp.wait()
 
 
 def products(b, f_alt, aux):
@@ -556,16 +551,26 @@
     width = rows // STEPS
     out = lambda *shape: jax.ShapeDtypeStruct(shape, F32)
     whole = pl.BlockSpec(memory_space=pltpu.VMEM)
+    hbm = pl.BlockSpec(memory_space=pl.ANY)
     return pl.pallas_call(
         product_kernel,
         name="products",
-        grid=(STEPS,),
         out_shape=(out(N, rows), out(W, rows), out(NP, W), out(NP, W, W)),
-        in_specs=[pl.BlockSpec((N, width), lambda i: (0, i)), pl.BlockSpec(memory_space=pl.ANY), whole],
-        out_specs=(pl.BlockSpec((N, width), lambda i: (0, i)), pl.BlockSpec((W, width), lambda i: (0, i)), whole, whole),
-        scratch_shapes=[pltpu.SemaphoreType.DMA],
+        in_specs=[whole, whole, whole],
+        out_specs=(hbm, hbm, whole, whole),
+        scratch_shapes=[pltpu.VMEM((N, width), F32), pltpu.VMEM((W, width), F32), pltpu.SemaphoreType.DMA((2, STEPS))],
         compiler_params=pltpu.CompilerParams(vmem_limit_bytes=32 * 1024 * 1024),
     )(b, f_alt, aux)
+
+
+def same_kernel(tau_in, t_in, tau_ref, t_ref):
+    tau_ref[...] = tau_in[...]
+    t_ref[...] = t_in[...]
+
+
+def row_major(tau_vals, t_fac):
+    out = lambda x: jax.ShapeDtypeStruct(x.shape, F32)
+    return pl.pallas_call(same_kernel, name="row_major", out_shape=(out(tau_vals), out(t_fac)))(tau_vals, t_fac)
 
 
 def all_pieces(x, axis, n):
@@ -701,10 +706,11 @@
 
         def again(state):
             factored, tau_new, t_new, q_new = careful(a_loc)
-            return jnp.zeros((1,), F32), q_new.T, factored.reshape(rows_loc, W).T, pack_aux(tau_new, t_new)
-
-        b, f_alt, aux = lax.while_loop(lambda s: s[0][0] > 0.5, again, (flag, b, f_alt, aux))[1:]
-        q_t, f_t, tau_vals, t_fac = products(b, f_alt, aux)
+            tau_new, t_new = row_major(tau_new, t_new)
+            return jnp.zeros((1,), F32), q_new.T, factored.reshape(rows_loc, W).T, tau_new, t_new
+
+        state = (flag,) + tuple(products(b, f_alt, aux))
+        q_t, f_t, tau_vals, t_fac = lax.while_loop(lambda s: s[0][0] > 0.5, again, state)[1:]
         return f_t.T.reshape(rows_loc, 1, W), tau_vals, t_fac, q_t.T
 
     spec_rows = P(("part", "row"), "col", None)

time: 70.5 us -> 65.9 us (0.935)
  Pallas kernels: 68.7 us -> 64.3 us
    pallas_call x1, Pallas kernels: 6.57 us -> 3.15 us  [products(): pl.pallas_call(product_kernel, name='products', out_shape=(out(N, rows),...]
    pallas_call x1, Pallas kernels: 62.1 us -> 61.1 us  [gather_and_factor(): pl.pallas_call(gather_kernel, name='gather_and_factor', out_shape=(out(N,...]
where the time goes in v4:
time: 65.9 us; the launch traced here: 65.8 us
  Pallas kernels  64.3 us (98%)
  between operations  0.81 us (1%)
  loops' own time  0.69 us (1%)
    pallas_call x1, Pallas kernels, gather_and_factor(): pl.pallas_call(gather_kernel, name='gather_and_factor', out_shape=(out(N,...  61.1 us
    pallas_call x1, Pallas kernels, products(): pl.pallas_call(product_kernel, name='products', out_shape=(out(N, rows),...  3.15 us

profile of v4, /device:TPU:0, one launch (start us, length us, event | category | flops | bytes accessed | tf_op | source)
XLA Modules:
  0.0 65.8 jit_solution(1023344917135721509)
XLA Ops:
  0.6 61.1 %gather_and_factor.1 = (f32[192,4096]{1,0:T(8,128)S(1)}, f32[48,4096]{1,0:T(8,128)S(1)}, f32[440,256]{1,0:T(8,128)S(1)}, f32[1]{0:T(128)}) custom-call(f32[48,4096]{1,0:T(8,128)} %bitcast.49.a_hbm), custom_call_target="tpu_custom_call" | custom-call | tf_op jit(solution)/shard_map/gather_and_factor/pallas_call | solution.py:504
  61.8 3.1 %products.1 = (f32[192,4096]{1,0:T(8,128)}, f32[48,4096]{1,0:T(8,128)}, f32[4,48]{1,0:T(4,128)}, f32[4,48,48]{2,1,0:T(8,128)}) custom-call(f32[192,4096]{1,0:T(8,128)S(1)} %get-tuple-element.729.b_ref, f32[48,4096]{1,0:T(8,128)S(1)} %get-tuple-element.730.f_alt, f32[440,256]{1,0:T(8,128)S(1)} %get-tuple-element.731.aux_ref), custom_call_target="tpu_custom_call" | custom-call | tf_op jit(solution)/shard_map/products/pallas_call | solution.py:555
  64.9 0.7 %while.138 = (f32[1]{0:T(128)}, f32[192,4096]{1,0:T(8,128)}, f32[48,4096]{1,0:T(8,128)}, f32[4,48]{1,0:T(4,128)}, f32[4,48,48]{2,1,0:T(8,128)}, /*index=5*/f32[4096,1,48]{0,2,1:T(8,128)}) while((f32[1]{0:T(128)}, f32[192,4096]{1,0:T(8,128)}, f32[48,4096]{1,0:T(8,128)}, f32[4,48]{1,0:T(4,128)}, f32[4,48,48]{2,1,0:T(8,128)}, ...), condition=%region_9.10_spmd, body=%region_0.9_spmd | while | flops 581720192 | bytes 76352704 | solution.py:713
